TPU v7x, 512 devices: a whole 4x8x8 slice. The times are simulated.
512 devices in a mesh: gx: 16 (over z, core), gy: 4 (over x), gz: 8 (over y).
Axes of the slice: x: 4, y: 8, z: 8, core: 2. Of those that a mesh axis runs over, the one named last changes fastest.
Arguments:
- krylov_basis: float32 [60, 64, 32, 1024], P(None, 'gx', 'gy', 'gz'), may hold values from -6 to 6
- schur_vectors: float32 [60, 20], replicated, may hold values from -1 to 1, as said below
- next_vector: float32 [64, 32, 1024], P('gx', 'gy', 'gz'), may hold values from -10 to 10
- diag_shift: float32 [64, 32, 1024], P('gx', 'gy', 'gz'), may hold values from 0.25 to 2
- velocity: float32 [3, 64, 32, 1024], P(None, 'gx', 'gy', 'gz'), may hold values from -1 to 1
Outputs:
- new_basis: float32 [24, 64, 32, 1024], P(None, 'gx', 'gy', 'gz')
- hessenberg: float32 [24, 3], replicated
Inputs may be any that keep to these rules, and one draw needn't show every extreme that they name: `schur_vectors`: the columns are orthonormal.
All inputs are finite; a program needn't handle non-finite values.
Results may differ from a plain program's by a relative error of at most 0.0003.
Values sent between devices are 32-bit elements; how exact they have to be, the bound alone decides.
A program may use at most 64 MiB of HBM per device.

v0:
```python
import functools

import jax
import jax.numpy as jnp
from jax import lax
from jax.experimental import pallas as pl
from jax.experimental.pallas import tpu as pltpu
from jax.sharding import PartitionSpec as P

KEEP = 20
EXPAND = 3
ROWS = 24
LANES = 128
UNIT = 16
DIRECT = 64
AXES = ("gx", "gy", "gz")


def partner_steps(phase, sizes):
    xs = range(1, sizes[0]) if phase else ()
    steps = [(dx, 0, 0) for dx in xs] if phase == 1 else [
        (dx, dy, dz) for dx in tuple(reversed(xs)) + (0,)
        for dy in range(sizes[1]) for dz in range(sizes[2])]
    return [step for step in steps if step != (0, 0, 0)]


def body(
    sizes, cells,
    kry_hbm, schur_hbm, w_hbm, diag_hbm, vel_hbm,
    out, hess,
    schur, w_ref, diag, vel, kry, image, xr, yr, zr, ypack, zpack, xh, yh, zh, xs, ys, zs,
    gsend, grecv0, grecv1, rsend, rrecv0, rrecv1, mid,
    load_sem, halo_send, halo_recv, gsem_s0, gsem_r0, gsem_s1, gsem_r1,
    rsem_s0, rsem_r0, rsem_s1, rsem_r1, ready,
):
    place = tuple(lax.axis_index(a) for a in AXES)
    basis = kry.shape[0]
    bx, by, bz = w_ref.shape
    loads = [
        pltpu.make_async_copy(source, target, load_sem.at[k])
        for k, (source, target) in enumerate((
            (w_hbm, w_ref), (schur_hbm, schur), (kry_hbm, kry), (diag_hbm, diag), (vel_hbm, vel)))
    ]
    for copy in loads:
        copy.start()
    direct = sizes[0] * sizes[1] * sizes[2] <= DIRECT
    shifted = [[lax.rem(place[d] + k, sizes[d]) for k in range(sizes[d])] for d in range(3)]

    def partners(phase):
        return [tuple(shifted[d][step[d]] for d in range(3))
                for step in partner_steps(phase, sizes)]


    for ref in (xr, yr, zr, xs, ys, zs):
        ref[...] = jnp.zeros_like(ref)

    barrier = pltpu.get_barrier_semaphore()
    for to in partners(0) + partners(1):
        pl.semaphore_signal(
            barrier, inc=1, device_id=to, device_id_type=pl.DeviceIdType.MESH)
    pl.semaphore_wait(barrier, len(partners(0)) + len(partners(1)))

    def halo_copies(kind, sources, targets):
        found = []
        for d in range(3):
            for side in (0, 1):
                at = (kind * 3 + d) * 2 + side
                to = list(place)
                to[d] = place[d] + (1 if side == 0 else -1)
                can_send = place[d] < sizes[d] - 1 if side == 0 else place[d] > 0
                can_recv = place[d] > 0 if side == 0 else place[d] < sizes[d] - 1
                found.append((
                    pltpu.make_async_remote_copy(
                        src_ref=sources[d][side], dst_ref=targets[d][side],
                        send_sem=halo_send.at[at], recv_sem=halo_recv.at[at],
                        device_id=tuple(to), device_id_type=pl.DeviceIdType.MESH,
                    ), can_send, can_recv))
        return found

    def halo_start(copies):
        for copy, can_send, _ in copies:
            pl.when(can_send)(copy.start)

    def halo_wait(copies):
        for copy, _, can_recv in copies:
            pl.when(can_recv)(copy.wait_recv)

    def halo_finish(copies):
        for copy, can_send, _ in copies:
            pl.when(can_send)(copy.wait_send)

    def field_copies(kind, ref):
        return halo_copies(
            kind,
            ((ref.at[bx - 1], ref.at[0]), (ref, ref), (ref, ref)),
            tuple((r.at[kind, 0], r.at[kind, 1]) for r in (xs, ys, zs)),
        )

    def exchange(send, slots, sem_s, sem_r, phase):
        for at, to in enumerate(partners(phase)):
            pltpu.make_async_remote_copy(
                src_ref=send, dst_ref=slots.at[at], send_sem=sem_s, recv_sem=sem_r,
                device_id=to, device_id_type=pl.DeviceIdType.MESH,
            ).start()
        pending.append(pltpu.make_async_copy(slots, slots, sem_s))
        return pltpu.make_async_copy(slots, slots, sem_r)

    def gather_sum(arrival, own, slots):
        arrival.wait()
        terms = [own] + [slots[k] for k in range(slots.shape[0])]
        while len(terms) > 1:
            terms = [sum(terms[k + 1:k + 2], terms[k]) for k in range(0, len(terms), 2)]
        return terms[0]

    pending = []

    def finish_sends():
        while pending:
            pending.pop().wait()

    def row_start(k, rowform):
        rsend[k] = rowform
        return exchange(rsend.at[k], rrecv0.at[k], rsem_s0.at[k], rsem_r0.at[k],
                        2 if direct else 0)

    def row_end(k, rowform, arrival):
        rowform = gather_sum(arrival, rowform, rrecv0.at[k])
        if not direct:
            mid[k] = rowform
            arrival = exchange(mid.at[k], rrecv1.at[k], rsem_s1.at[k], rsem_r1.at[k], 1)
            rowform = gather_sum(arrival, rowform, rrecv1.at[k])
        return rowform * (1.0 / cells)

    lane3 = lax.broadcasted_iota(jnp.int32, (by, bz), 1)
    row3 = lax.broadcasted_iota(jnp.int32, (by, bz), 0)

    def stencil(v, x_before, x_after, y_before, y_after, z_before, z_after):
        res = []
        for x in range(bx):
            here = v[x]
            xb = v[x - 1] if x > 0 else x_before
            xa = v[x + 1] if x < bx - 1 else x_after
            yb = jnp.where(row3 == 0, y_before[x], pltpu.roll(here, 1, 0))
            ya = jnp.where(row3 == by - 1, y_after[x], pltpu.roll(here, by - 1, 0))
            zb = jnp.where(lane3 == 0, z_before[x], pltpu.roll(here, 1, 1))
            za = jnp.where(lane3 == bz - 1, z_after[x], pltpu.roll(here, bz - 1, 1))
            neighbours = xa + xb + ya + yb + za + zb
            flow = (vel[0, x] * (xa - xb) + vel[1, x] * (ya - yb) + vel[2, x] * (za - zb))
            res.append((6.0 + diag[x]) * here - neighbours + 0.5 * flow)
        return res

    def dots(v, count, first=0):
        parts = []
        for i in range(ROWS):
            if first <= i < count:
                total = out[i, 0] * v[0]
                for x in range(1, bx):
                    total = total + out[i, x] * v[x]
            elif i == ROWS - 1:
                total = v[0] * v[0]
                for x in range(1, bx):
                    total = total + v[x] * v[x]
            else:
                total = None
            parts.append(jnp.zeros((1, bz), jnp.float32) if total is None
                         else jnp.sum(total, axis=0, keepdims=True))
        return jnp.sum(jnp.concatenate(parts, axis=0), axis=1, keepdims=True)

    halo_w = field_copies(0, w_ref)
    loads[0].wait()
    halo_start(halo_w)
    if direct:
        for to in partners(1):
            pl.semaphore_signal(
                ready, inc=1, device_id=to, device_id_type=pl.DeviceIdType.MESH)

    out[KEEP + 1:ROWS] = jnp.zeros((ROWS - KEEP - 1, bx, by, bz), jnp.float32)
    out[KEEP] = w_ref[...]
    loads[1].wait()
    loads[2].wait()
    wide, deep = 5, 4
    for first in range(0, KEEP, wide):
        def step(at, sums, first=first):
            sums = list(sums)
            for k in range(deep):
                i = at * deep + k
                for x in range(bx):
                    tile = kry[i, x]
                    for j in range(wide):
                        sums[j * bx + x] = sums[j * bx + x] + schur[first + j, i] * tile
            return tuple(sums)
        sums = lax.fori_loop(
            0, basis // deep, step,
            tuple(jnp.zeros((by, bz), jnp.float32) for _ in range(wide * bx)))
        for j in range(wide):
            for x in range(bx):
                out[first + j, x] = sums[j * bx + x]

    row = lax.broadcasted_iota(jnp.int32, (ROWS, LANES), 0)
    lane = lax.broadcasted_iota(jnp.int32, (ROWS, LANES), 1)
    lane1 = lax.broadcasted_iota(jnp.int32, (1, LANES), 1)
    row1 = lax.broadcasted_iota(jnp.int32, (ROWS, 1), 0)

    gram = jnp.zeros((ROWS, LANES), jnp.float32)
    for j in range(KEEP + 1):
        col = dots([out[j, x] for x in range(bx)], KEEP + 1, j // 8 * 8)
        gram = jnp.where((lane == j) & (row < KEEP + 1), col, gram)
    lane8 = lax.broadcasted_iota(jnp.int32, (8, LANES), 1)
    own8 = lane8 // UNIT == lax.broadcasted_iota(jnp.int32, (8, LANES), 0)

    def spread(value):
        for shift in (UNIT, 2 * UNIT, 4 * UNIT):
            value = value + pltpu.roll(value, shift, 1)
        return value

    units = (
        gram[16:24],
        gram[8:16],
        jnp.where(lane8 < 8, gram[0:8], pltpu.roll(gram[16:24], LANES - 8, 1)),
    )
    packed = jnp.concatenate([
        jnp.sum(jnp.where(own8, spread(jnp.where(lane8 < UNIT, unit, 0.0)), 0.0),
                axis=0, keepdims=True)
        for unit in units], axis=0)
    gsend[0] = packed
    if direct:
        pl.semaphore_wait(ready, sizes[0] - 1)
    arrival0 = exchange(gsend.at[0], grecv1, gsem_s1, gsem_r1, 2 if direct else 1)

    loads[3].wait()
    loads[4].wait()
    halo_wait(halo_w)
    applied = stencil(
        [w_ref[x] for x in range(bx)], xs[0, 0], xs[0, 1],
        [ys[0, 0, x, by - 1:by, :] for x in range(bx)],
        [ys[0, 1, x, 0:1, :] for x in range(bx)],
        [zs[0, 0, x, :, bz - 1:bz] for x in range(bx)],
        [zs[0, 1, x, :, 0:1] for x in range(bx)],
    )
    for x in range(bx):
        image[0, x] = applied[x]
    ownrow = jnp.sum(jnp.where(row == lane, dots(applied, KEEP + 1), 0.0),
                     axis=0, keepdims=True)
    copies = row_start(0, ownrow)
    halo_a = field_copies(1, image.at[0])
    halo_start(halo_a)

    for side, (near, edge) in enumerate(((by - 1, bz - 1), (0, 0))):
        for i in range(KEEP):
            ypack[side, i] = out[i, :, near, :]
        for x in range(bx):
            face = jnp.zeros((by, bz), jnp.float32)
            for i in range(KEEP):
                face = jnp.where(
                    lane3 == i, pltpu.roll(out[i, x], (i - edge) % bz, 1), face)
            zpack[side, x] = face
    halo_r = halo_copies(
        3,
        ((out.at[0:KEEP, bx - 1], out.at[0:KEEP, 0]), (ypack.at[0], ypack.at[1]),
         (zpack.at[0], zpack.at[1])),
        tuple((r.at[0], r.at[1]) for r in (xr, yr, zr)),
    )
    halo_start(halo_r)

    packed = gather_sum(arrival0, packed, grecv1)
    if not direct:
        gsend[1] = packed
        arrival1 = exchange(gsend.at[1], grecv0, gsem_s0, gsem_r0, 0)
        packed = gather_sum(arrival1, packed, grecv0)
    packed = packed * (1.0 / cells)
    units = [
        jnp.where(lane8 < UNIT,
                  spread(jnp.where(own8, jnp.broadcast_to(packed[u:u + 1], (8, LANES)), 0.0)),
                  0.0)
        for u in range(3)]
    corner = pltpu.roll(jnp.where(lane8 >= 8, units[2], 0.0), 8, 1)
    below = jnp.concatenate(
        [jnp.zeros((8, LANES), jnp.float32), jnp.where(lane8 < 8, units[1], 0.0), units[0],
         jnp.zeros((LANES - ROWS, LANES), jnp.float32)], axis=0)
    gram = jnp.concatenate(
        [jnp.where(lane8 < 8, units[2], 0.0), units[1], units[0] + corner], axis=0)
    gram = gram + below.T[0:ROWS]
    gram = jnp.where((lane < KEEP + 1) & (row < KEEP + 1), gram, 0.0)
    norm_sq = jnp.sum(
        jnp.sum(jnp.where((lane == KEEP) & (row == KEEP), gram, 0.0), axis=1, keepdims=True),
        axis=0, keepdims=True)
    scale = 1.0 / jnp.maximum(jnp.sqrt(norm_sq), 0.5)
    gram = gram * jnp.where(row == KEEP, scale, 1.0) * jnp.where(lane == KEEP, scale, 1.0)
    for x in range(bx):
        out[KEEP, x] = w_ref[x] * scale
    applied = [tile * scale for tile in applied]
    rowform = row_end(0, ownrow, copies)
    rowform = rowform * scale * jnp.where((lane1 == KEEP) | (lane1 == ROWS - 1), scale, 1.0)

    halo_wait(halo_r)
    for side in (0, 1):
        near_row, near_lane = (by - 1, bz - 1) if side == 0 else (0, 0)
        xh[side, 0] = xs[0, side] * scale
        for x in range(bx):
            yh[side, 0, x:x + 1] = ys[0, side, x, near_row:near_row + 1, :] * scale
            zh[side, x] = jnp.where(
                lane3 == KEEP, zs[0, side, x, :, near_lane:near_lane + 1] * scale, zr[side, x])
    halos = {1: halo_a}
    done = [halo_w, halo_r, halo_a]
    hcols = []
    for k in range(EXPAND):
        count = KEEP + 1 + k
        if k > 0:
            rowform = jnp.sum(jnp.where(row == lane, dots(applied, count), 0.0),
                              axis=0, keepdims=True)
            earlier = pending[:]
            pending.clear()
            arrival = row_start(k, rowform)
            for copy in earlier:
                copy.wait()
            for copies in done:
                halo_finish(copies)
            done = []
            rowform = row_end(k, rowform, arrival)
        c_row = jnp.where(lane1 < count, rowform, 0.0)
        twice = jnp.where(row == lane, 2.0, 0.0) - gram
        t_col = jnp.sum(twice * c_row, axis=1, keepdims=True)
        weights = jnp.broadcast_to(t_col, (ROWS, LANES))
        t_row = jnp.sum(jnp.where(row == lane, weights, 0.0), axis=0, keepdims=True)
        gt_row = jnp.sum(gram * weights, axis=0, keepdims=True)
        length_sq = jnp.sum(
            jnp.where(lane1 == ROWS - 1, rowform, t_row * (gt_row - 2.0 * c_row)),
            axis=1, keepdims=True)
        length_sq = jnp.maximum(length_sq, 0.0)
        length = jnp.sqrt(length_sq)
        inverse = 1.0 / jnp.maximum(length, 0.5)
        hcols.append(jnp.where(lane1 == count, length, t_row))
        newest = list(applied)
        for i in range(count):
            weight = jnp.broadcast_to(weights[i:i + 1, :], (by, bz))
            for x in range(bx):
                newest[x] = newest[x] - weight * out[i, x]
        newest = [tile * inverse for tile in newest]
        for x in range(bx):
            out[count, x] = newest[x]
        if k == EXPAND - 1:
            break
        halo_wait(halos[k + 1])
        sides = []
        for side in (0, 1):
            near_row, near_lane = (by - 1, bz - 1) if side == 0 else (0, 0)
            factor = scale if k == 0 else 1.0
            x_part = xs[k + 1, side] * factor
            y_part = [ys[k + 1, side, x, near_row:near_row + 1, :] * factor for x in range(bx)]
            y_part = jnp.concatenate(y_part, axis=0)
            for i in range(count):
                weight = weights[i:i + 1, :]
                if i < KEEP:
                    x_part = x_part - weight * xr[side, i]
                    y_part = y_part - weight * yr[side, i]
                else:
                    x_part = x_part - weight * xh[side, i - KEEP]
                    y_part = y_part - weight * yh[side, i - KEEP]
            x_part = x_part * inverse
            y_part = y_part * inverse
            z_part = []
            for x in range(bx):
                column = (zs[k + 1, side, x, :, near_lane:near_lane + 1] * factor
                          - jnp.sum(zh[side, x] * t_row, axis=1, keepdims=True)) * inverse
                z_part.append(column)
                if k + 1 < EXPAND - 1:
                    zh[side, x] = jnp.where(lane3 == count, column, zh[side, x])
            xh[side, count - KEEP] = x_part
            yh[side, count - KEEP] = y_part
            sides.append((x_part, [y_part[x:x + 1] for x in range(bx)], z_part))
        applied = stencil(newest, sides[0][0], sides[1][0], sides[0][1], sides[1][1],
                          sides[0][2], sides[1][2])
        if k + 1 < EXPAND - 1:
            for x in range(bx):
                image[1, x] = applied[x]
            halos[k + 2] = field_copies(k + 2, image.at[1])
            halo_start(halos[k + 2])
            done.append(halos[k + 2])
        e_row = t_row - c_row
        e_col = jnp.sum(jnp.where(row == lane, e_row, 0.0), axis=1, keepdims=True)
        cross_col = (e_col - jnp.sum(gram * e_row, axis=1, keepdims=True)) * inverse
        cross_row = (e_row - jnp.sum(gram * e_col, axis=0, keepdims=True)) * inverse
        corner = length_sq * inverse * inverse
        gram = jnp.where(row == count, cross_row, jnp.where(lane == count, cross_col, gram))
        gram = jnp.where((row == count) & (lane == count), corner, gram)

    for k in range(EXPAND):
        hess[k:k + 1] = hcols[k % len(hcols)]
    for copies in done:
        halo_finish(copies)
    finish_sends()


def per_device(krylov_basis, schur_vectors, next_vector, diag_shift, velocity):
    sizes = tuple(lax.axis_size(a) for a in AXES)
    block = next_vector.shape
    bx, by, bz = block
    cells = float(bx * by * bz * sizes[0] * sizes[1] * sizes[2])
    n0, n1 = sizes[1] * sizes[2], sizes[0]
    nrow = n0 * n1 if n0 * n1 <= DIRECT else n0
    nline = n0 * n1 if n0 * n1 <= DIRECT else n1
    f32 = jnp.float32
    vmem = pl.BlockSpec(memory_space=pltpu.VMEM)
    dma = pltpu.SemaphoreType.DMA
    vectors, columns = pl.pallas_call(
        functools.partial(body, sizes, cells),
        out_shape=(
            pltpu.VMEM((ROWS,) + block, f32),
            pltpu.VMEM((8, LANES), f32),
        ),
        in_specs=[
            pl.BlockSpec(memory_space=pl.ANY) for _ in range(5)
        ],
        out_specs=(vmem, vmem),
        scratch_shapes=[
            pltpu.SMEM(schur_vectors.shape[::-1], f32),
            pltpu.VMEM(block, f32),
            pltpu.VMEM(block, f32),
            pltpu.VMEM((3,) + block, f32),
            pltpu.VMEM(krylov_basis.shape, f32),
            pltpu.VMEM((2,) + block, f32),
            pltpu.VMEM((2, KEEP, by, bz), f32),
            pltpu.VMEM((2, KEEP, bx, bz), f32),
            pltpu.VMEM((2,) + block, f32),
            pltpu.VMEM((2, KEEP, bx, bz), f32),
            pltpu.VMEM((2,) + block, f32),
            pltpu.VMEM((2, EXPAND, by, bz), f32),
            pltpu.VMEM((2, EXPAND, bx, bz), f32),
            pltpu.VMEM((2,) + block, f32),
            pltpu.VMEM((EXPAND, 2, by, bz), f32),
            pltpu.VMEM((EXPAND, 2) + block, f32),
            pltpu.VMEM((EXPAND, 2) + block, f32),
            pltpu.VMEM((2, 3, LANES), f32),
            pltpu.VMEM((n0 - 1, 3, LANES), f32),
            pltpu.VMEM((nline - 1, 3, LANES), f32),
            pltpu.VMEM((EXPAND, 1, LANES), f32),
            pltpu.VMEM((EXPAND, nrow - 1, 1, LANES), f32),
            pltpu.VMEM((EXPAND, n1 - 1, 1, LANES), f32),
            pltpu.VMEM((EXPAND, 1, LANES), f32),
            dma((5,)), dma((24,)), dma((24,)),
            dma, dma, dma, dma,
            dma((EXPAND,)), dma((EXPAND,)), dma((EXPAND,)), dma((EXPAND,)),
            pltpu.SemaphoreType.REGULAR,
        ],
        compiler_params=pltpu.CompilerParams(collective_id=0, has_side_effects=True),
    )(krylov_basis, schur_vectors.T, next_vector, diag_shift, velocity)
    return vectors, columns[0:EXPAND, 0:ROWS].T


def solution(mesh):
    in_specs = (
        P(None, "gx", "gy", "gz"),
        P(),
        P("gx", "gy", "gz"),
        P("gx", "gy", "gz"),
        P(None, "gx", "gy", "gz"),
    )
    out_specs = (P(None, "gx", "gy", "gz"), P())
    return jax.shard_map(
        per_device, mesh=mesh, in_specs=in_specs, out_specs=out_specs, check_vma=False
    )
```

profile of v0, /device:TPU:1, one launch (start us, length us, event | category | flops | bytes accessed | tf_op | source)
XLA Modules:
  0.0 58.4 jit_solution(11409816026163334497)
XLA Ops:
  0.6 56.5 %shard_map.68 = (f32[24,4,8,128]{3,2,1,0:T(8,128)S(1)}, f32[8,128]{1,0:T(8,128)S(1)}) custom-call(f32[60,4,8,128]{3,2,1,0:T(8,128)} %kry_hbm.1, f32[20,60]{1,0:T(8,128)} %bitcast.3, f32[4,8,128]{2,1,0:T(8,128)} %w_hbm.1, f32[4,8,128]{2,1,0:T(8,128)} %diag_hbm.1, f32[3,4,8,128]{3,2,1,0:T(8,128)} %vel_hbm.1), custom_call_target="tpu_custom_call" | custom-call | tf_op jit(solution)/shard_map/pallas_call | solution.py:405
  57.1 0.7 %copy.8 = f32[24,4,8,128]{3,2,1,0:T(8,128)} copy(f32[24,4,8,128]{3,2,1,0:T(8,128)S(1)} %get-tuple-element.6) | data formatting | bytes 786432
  57.9 0.6 slice_bitcast_fusion
where the time goes:
time: 58.6 us; the launch traced here: 58.4 us
  Pallas kernels  56.5 us (96%)
  local copies, waits for them, and re-layouts  1.33 us (2%)
  between operations  0.64 us (1%)
    pallas_call x1, Pallas kernels, per_device(): pl.pallas_call(functools.partial(body, sizes, cells), out_shape=(pltpu.VM...  56.5 us

commit v1 on v0

v1 whole, which is shorter than its diff:
```python
import functools

import jax
import jax.numpy as jnp
from jax import lax
from jax.experimental import pallas as pl
from jax.experimental.pallas import tpu as pltpu
from jax.sharding import PartitionSpec as P

KEEP = 20
EXPAND = 3
ROWS = 24
LANES = 128
UNIT = 16
PITCH = 40
AXES = ("gx", "gy", "gz")


def partner_steps(phase, sizes):
    if phase == 1:
        return [(dx, 0, 0) for dx in range(1, sizes[0])]
    return [(0, dy, dz) for dy in range(sizes[1]) for dz in range(sizes[2])][1:]


def body(
    sizes, cells,
    kry_hbm, schur_hbm, w_hbm, diag_hbm, vel_hbm,
    out, hess,
    schur, w_ref, diag, vel, kry, coef, t0, t1, t2, wrow, image,
    xs, ys, zs, xh, yh, zh, zpack, split0, split1,
    gsend, grecv0, grecv1, bsend, brecv0, brecv1, rsend, rrecv0, rrecv1,
    load_sem, halo_send, halo_recv, red_send, red_recv,
):
    f32, bf16 = jnp.float32, jnp.bfloat16
    place = tuple(lax.axis_index(a) for a in AXES)
    basis = kry_hbm.shape[0]
    bx, by, bz = w_ref.shape
    area = bx * by
    loads = [
        pltpu.make_async_copy(source, target, load_sem.at[k])
        for k, (source, target) in enumerate((
            (w_hbm, w_ref), (kry_hbm, kry_hbm), (schur_hbm, schur),
            (diag_hbm, diag), (vel_hbm, vel)))
    ]
    for copy in loads[:1] + loads[2:]:
        copy.start()
    for i in range(basis):
        pltpu.make_async_copy(
            kry_hbm.at[i], kry.at[pl.ds(i * PITCH, area)], load_sem.at[1]).start()
    shifted = [[lax.rem(place[d] + k, sizes[d]) for k in range(sizes[d])] for d in range(3)]

    def partners(phase):
        return [tuple(shifted[d][step[d]] for d in range(3))
                for step in partner_steps(phase, sizes)]

    barrier = pltpu.get_barrier_semaphore()
    for to in partners(0) + partners(1):
        pl.semaphore_signal(
            barrier, inc=1, device_id=to, device_id_type=pl.DeviceIdType.MESH)

    for d, slots in enumerate(((xs, xh), (ys, yh), (zs, zh))):
        for side in (0, 1):
            def clear(slots=slots, side=side):
                for ref in slots:
                    for k in range(ref.shape[0]):
                        ref[k, side] = jnp.zeros(ref.shape[2:], f32)
            pl.when(place[d] == (0 if side == 0 else sizes[d] - 1))(clear)

    def halo_copies(kind, sources, targets):
        found = []
        for d in range(3):
            for side in (0, 1):
                at = (kind * 3 + d) * 2 + side
                to = list(place)
                to[d] = place[d] + (1 if side == 0 else -1)
                can_send = place[d] < sizes[d] - 1 if side == 0 else place[d] > 0
                can_recv = place[d] > 0 if side == 0 else place[d] < sizes[d] - 1
                found.append((
                    pltpu.make_async_remote_copy(
                        src_ref=sources[d][side], dst_ref=targets[d][side],
                        send_sem=halo_send.at[at], recv_sem=halo_recv.at[at],
                        device_id=tuple(to), device_id_type=pl.DeviceIdType.MESH,
                    ), can_send, can_recv))
        return found

    def halo_start(copies):
        for copy, can_send, _ in copies:
            pl.when(can_send)(copy.start)

    def halo_wait(copies):
        for copy, _, can_recv in copies:
            pl.when(can_recv)(copy.wait_recv)

    def halo_finish(copies):
        for copy, can_send, _ in copies:
            pl.when(can_send)(copy.wait_send)

    def field_copies(kind, ref):
        return halo_copies(
            kind,
            ((ref.at[bx - 1], ref.at[0]), (ref, ref), (ref, ref)),
            tuple((r.at[kind, 0], r.at[kind, 1]) for r in (xs, ys, zs)),
        )

    def rows_copies(level, ref):
        return halo_copies(
            EXPAND + level,
            ((ref.at[bx - 1], ref.at[0]), (ref.at[:, by - 1], ref.at[:, 0]),
             (zpack.at[level, 0], zpack.at[level, 1])),
            tuple((r.at[level, 0], r.at[level, 1]) for r in (xh, yh, zh)),
        )

    pending = []

    def exchange(kind, send, slots, phase):
        at = kind * 2 + phase
        for k, to in enumerate(partners(phase)):
            pltpu.make_async_remote_copy(
                src_ref=send, dst_ref=slots.at[k], send_sem=red_send.at[at],
                recv_sem=red_recv.at[at],
                device_id=to, device_id_type=pl.DeviceIdType.MESH,
            ).start()
        pending.append(pltpu.make_async_copy(slots, slots, red_send.at[at]))
        return pltpu.make_async_copy(slots, slots, red_recv.at[at])

    def gather_sum(arrival, own, slots):
        arrival.wait()
        terms = [own] + [slots[k] for k in range(slots.shape[0])]
        while len(terms) > 1:
            terms = [sum(terms[k + 1:k + 2], terms[k]) for k in range(0, len(terms), 2)]
        return terms[0]

    def reduce_start(kind, buffers, value):
        send, slots0, _ = buffers
        send[0] = value
        return value, exchange(kind, send.at[0], slots0, 0)

    def reduce_turn(kind, buffers, state):
        send, slots0, slots1 = buffers
        value = gather_sum(state[1], state[0], slots0)
        send[1] = value
        return value, exchange(kind, send.at[1], slots1, 1)

    def reduce_end(buffers, state):
        return gather_sum(state[1], state[0], buffers[2]) * (1.0 / cells)

    gram_buffers = (gsend, grecv0, grecv1)
    back_buffers = (bsend, brecv0, brecv1)
    row_buffers = (rsend, rrecv0, rrecv1)

    lane3 = lax.broadcasted_iota(jnp.int32, (by, bz), 1)
    row3 = lax.broadcasted_iota(jnp.int32, (by, bz), 0)
    lane24 = lax.broadcasted_iota(jnp.int32, (ROWS, bz), 1)

    def field_stencil(v, kind):
        res = []
        for x in range(bx):
            here = v[x]
            xb = v[x - 1] if x > 0 else xs[kind, 0]
            xa = v[x + 1] if x < bx - 1 else xs[kind, 1]
            yb = jnp.where(row3 == 0, ys[kind, 0, x, by - 1:by, :], pltpu.roll(here, 1, 0))
            ya = jnp.where(row3 == by - 1, ys[kind, 1, x, 0:1, :], pltpu.roll(here, by - 1, 0))
            zb = jnp.where(lane3 == 0, zs[kind, 0, x, :, bz - 1:bz], pltpu.roll(here, 1, 1))
            za = jnp.where(lane3 == bz - 1, zs[kind, 1, x, :, 0:1], pltpu.roll(here, bz - 1, 1))
            res.append(coef[6, x] * here + (coef[0, x] * xb + coef[1, x] * xa)
                       + (coef[2, x] * yb + coef[3, x] * ya)
                       + (coef[4, x] * zb + coef[5, x] * za))
        return res

    def rows_stencil(level, source, target):
        low, high = zh[level, 0], zh[level, 1]
        for x in range(bx):
            for y in range(by):
                at = x * by + y
                here = source[x, y]
                xb = source[x - 1, y] if x > 0 else xh[level, 0, y]
                xa = source[x + 1, y] if x < bx - 1 else xh[level, 1, y]
                yb = source[x, y - 1] if y > 0 else yh[level, 0, x]
                ya = source[x, y + 1] if y < by - 1 else yh[level, 1, x]
                zb = jnp.where(lane24 == 0, pltpu.roll(low, (bz - at) % bz, 1),
                               pltpu.roll(here, 1, 1))
                za = jnp.where(lane24 == bz - 1, pltpu.roll(high, bz - 1 - at, 1),
                               pltpu.roll(here, bz - 1, 1))
                c = [coef[k, x, y:y + 1, :] for k in range(7)]
                target[x, y] = (c[6] * here + (c[0] * xb + c[1] * xa)
                                + (c[2] * yb + c[3] * ya) + (c[4] * zb + c[5] * za))

    def pack_faces(level, source):
        for side, edge in enumerate((bz - 1, 0)):
            face = jnp.zeros((ROWS, bz), f32)
            for x in range(bx):
                for y in range(by):
                    at = x * by + y
                    face = jnp.where(
                        lane24 == at, pltpu.roll(source[x, y], (at - edge) % bz, 1), face)
            zpack[level, side] = face

    def put_row(k, tiles):
        for x in range(bx):
            wrow[pl.ds(x * by * 8 + 4 + k, by, stride=8), :] = tiles[x]

    def tail(x, y):
        return t0[x, y, 16:24] + wrow[(x * by + y) * 8:(x * by + y) * 8 + 8]

    def first_block(x, y):
        return [t0[x, y, 0:8], t0[x, y, 8:16], tail(x, y)]

    def second_block(x, y):
        return [t1[x, y, 0:8], t1[x, y, 8:16], t1[x, y, 16:24]]

    def put_split(ref, p, u):
        n = u.shape[0]
        at = pl.ds(p * 2 * bz, 2 * bz)
        high = u.astype(bf16)
        rest = u - high.astype(f32)
        mid = rest.astype(bf16)
        ref[0:n, at] = high
        ref[n:2 * n, at] = mid
        ref[2 * n:3 * n, at] = (rest - mid.astype(f32)).astype(bf16)

    def both(block, p):
        return [jnp.concatenate([block(*divmod(2 * p, by))[k], block(*divmod(2 * p + 1, by))[k]],
                                axis=1) for k in range(3)]

    dot_nt = functools.partial(
        lax.dot_general, dimension_numbers=(((1,), (1,)), ((), ())), preferred_element_type=f32)

    halo_w = field_copies(0, w_ref)
    wrow[...] = jnp.zeros_like(wrow)
    t0[:, :, 16:24] = jnp.zeros((bx, by, 8, bz), f32)
    split0[96:128] = jnp.zeros((32, split0.shape[1]), bf16)
    loads[0].wait()
    pl.semaphore_wait(barrier, len(partners(0)) + len(partners(1)))
    halo_start(halo_w)
    w = [w_ref[x] for x in range(bx)]
    put_row(0, w)

    loads[2].wait()
    loads[1].wait()
    turn = schur[...]
    turn_high = turn.astype(bf16)
    turn_low = (turn - turn_high.astype(f32)).astype(bf16)
    for p in range(area // 2):
        u = jnp.concatenate([kry[pl.ds(2 * p, basis, stride=PITCH), :],
                             kry[pl.ds(2 * p + 1, basis, stride=PITCH), :]], axis=1)
        high = u.astype(bf16)
        low = (u - high.astype(f32)).astype(bf16)
        r = (jnp.dot(turn_high, high, preferred_element_type=f32)
             + (jnp.dot(turn_high, low, preferred_element_type=f32)
                + jnp.dot(turn_low, high, preferred_element_type=f32)))
        for k in (0, 1):
            x, y = divmod(2 * p + k, by)
            t0[x, y, 0:KEEP] = r[:, k * bz:(k + 1) * bz]
    pack_faces(0, t0)
    halo_r = rows_copies(0, t0)
    halo_start(halo_r)

    loads[3].wait()
    loads[4].wait()
    for x in range(bx):
        for d in range(3):
            half = 0.5 * vel[d, x]
            coef[2 * d, x] = -1.0 - half
            coef[2 * d + 1, x] = half - 1.0
        coef[6, x] = 6.0 + diag[x]
    halo_wait(halo_w)
    once = field_stencil(w, 0)
    for x in range(bx):
        image[0, x] = once[x]
    halo_a = field_copies(1, image.at[0])
    halo_start(halo_a)
    put_row(1, once)

    zero8 = jnp.zeros((8, 2 * bz), f32)
    for p in range(area // 2):
        put_split(split0, p, jnp.concatenate(both(first_block, p) + [zero8], axis=0))
    prod = dot_nt(split0[0:96], split0[...])
    prod = prod[0:24] + prod[32:56] + prod[64:88]
    gram = prod + pltpu.roll(prod, LANES - 32, 1) + pltpu.roll(prod, LANES - 64, 1)

    row = lax.broadcasted_iota(jnp.int32, (ROWS, LANES), 0)
    lane = lax.broadcasted_iota(jnp.int32, (ROWS, LANES), 1)
    lane1 = lax.broadcasted_iota(jnp.int32, (1, LANES), 1)
    row8 = lax.broadcasted_iota(jnp.int32, (8, LANES), 0)
    lane8 = lax.broadcasted_iota(jnp.int32, (8, LANES), 1)
    row48 = lax.broadcasted_iota(jnp.int32, (2 * ROWS, LANES), 0)
    lane48 = lax.broadcasted_iota(jnp.int32, (2 * ROWS, LANES), 1)
    own8 = lane8 // UNIT == row8

    def spread(value):
        for shift in (UNIT, 2 * UNIT, 4 * UNIT):
            value = value + pltpu.roll(value, shift, 1)
        return value

    units = (
        gram[16:24],
        gram[8:16],
        jnp.where(lane8 < 8, gram[0:8], pltpu.roll(gram[16:24], LANES - 8, 1)),
    )
    packed = jnp.concatenate([
        jnp.sum(jnp.where(own8, spread(jnp.where(lane8 < UNIT, unit, 0.0)), 0.0),
                axis=0, keepdims=True)
        for unit in units], axis=0)
    gram_state = reduce_start(0, gram_buffers, packed)

    halo_wait(halo_a)
    twice_w = field_stencil(once, 1)
    for x in range(bx):
        image[1, x] = twice_w[x]
    halo_b = field_copies(2, image.at[1])
    halo_start(halo_b)
    put_row(2, twice_w)
    halo_wait(halo_r)
    rows_stencil(0, t0, t1)
    pack_faces(1, t1)
    halo_t = rows_copies(1, t1)
    halo_start(halo_t)
    for p in range(area // 2):
        put_split(split1, p, jnp.concatenate(
            both(first_block, p) + both(second_block, p), axis=0))
    prod = dot_nt(split1[...], split1[...])
    prod = prod[0:48] + prod[48:96] + prod[96:144]
    left = prod[:, 0:LANES]
    right = jnp.concatenate(
        [prod[:, LANES:], jnp.zeros((48, 2 * LANES - prod.shape[1]), f32)], axis=1)
    cross = left + pltpu.roll(left, LANES - 48, 1) + jnp.where(
        lane48 < 32, pltpu.roll(left, LANES - 96, 1), pltpu.roll(right, 32, 1))

    places = ((0, 24, 0, 24), (8, 24, 24, 24), (16, 24, 48, 24), (24, 24, 72, 24),
              (32, 32, 96, 16), (40, 40, 112, 8), (0, 22, 120, 1), (8, 22, 121, 1), (16, 22, 122, 1))
    tile = jnp.zeros((8, LANES), f32)
    for top, source, target, width in places:
        tile = jnp.where((lane8 >= target) & (lane8 < target + width),
                         pltpu.roll(cross[top:top + 8], (target - source) % LANES, 1), tile)

    gram_state = reduce_turn(0, gram_buffers, gram_state)
    back_state = reduce_start(1, back_buffers, tile)
    for x in range(bx):
        for y in range(by):
            out[pl.ds(x * by + y, ROWS, stride=area), :] = t0[x, y]
    halo_wait(halo_b)
    put_row(3, field_stencil(twice_w, 2))
    halo_wait(halo_t)
    rows_stencil(1, t1, t2)

    packed = reduce_end(gram_buffers, gram_state)
    units = [
        jnp.where(lane8 < UNIT,
                  spread(jnp.where(own8, jnp.broadcast_to(packed[u:u + 1], (8, LANES)), 0.0)),
                  0.0)
        for u in range(3)]
    corner = pltpu.roll(jnp.where(lane8 >= 8, units[2], 0.0), 8, 1)
    below = jnp.concatenate(
        [jnp.zeros((8, LANES), f32), jnp.where(lane8 < 8, units[1], 0.0), units[0],
         jnp.zeros((LANES - ROWS, LANES), f32)], axis=0)
    known = jnp.concatenate(
        [jnp.where(lane8 < 8, units[2], 0.0), units[1], units[0] + corner], axis=0)
    known = known + below.T[0:ROWS]
    known = jnp.where((lane < KEEP + 2) & (row < KEEP + 2), known, 0.0)
    norm_sq = jnp.sum(
        jnp.sum(jnp.where((lane == KEEP) & (row == KEEP), known, 0.0), axis=1, keepdims=True),
        axis=0, keepdims=True)
    scale = 1.0 / jnp.maximum(jnp.sqrt(norm_sq), 0.5)
    gram = known * jnp.where(row == KEEP, scale, 1.0) * jnp.where(lane == KEEP, scale, 1.0)
    gram = jnp.where((lane < KEEP + 1) & (row < KEEP + 1), gram, 0.0)

    def assemble(form, *extra):
        form = jnp.where(lane1 < KEEP, form, jnp.where(lane1 == KEEP, form * scale, 0.0))
        for at, value in extra:
            form = jnp.where(lane1 == at, value, form)
        return form

    def pick(form, at):
        return jnp.sum(jnp.where(lane1 == at, form, 0.0), axis=1, keepdims=True)

    def column(form, count=2 * ROWS):
        own = row48[0:count] == lane48[0:count]
        return jnp.broadcast_to(
            jnp.sum(jnp.where(own, form, 0.0), axis=1, keepdims=True), (count, LANES))

    def applied(form):
        return pltpu.roll(jnp.where(lane1 < KEEP, form, 0.0), ROWS, 1) + jnp.where(
            (lane1 == KEEP + 1) | (lane1 == KEEP + 2), pltpu.roll(form, 1, 1), 0.0)

    hcols = []

    def arnoldi(rowform, gram, count, last=False):
        c_row = jnp.where(lane1 < count, rowform, 0.0)
        twice = jnp.where(row == lane, 2.0, 0.0) - gram
        t_col = jnp.sum(twice * c_row, axis=1, keepdims=True)
        weights = jnp.broadcast_to(t_col, (ROWS, LANES))
        t_row = jnp.sum(jnp.where(row == lane, weights, 0.0), axis=0, keepdims=True)
        gt_row = jnp.sum(gram * weights, axis=0, keepdims=True)
        length_sq = jnp.sum(
            jnp.where(lane1 == ROWS - 1, rowform, t_row * (gt_row - 2.0 * c_row)),
            axis=1, keepdims=True)
        length_sq = jnp.maximum(length_sq, 0.0)
        length = jnp.sqrt(length_sq)
        inverse = 1.0 / jnp.maximum(length, 0.5)
        hcols.append(jnp.where(lane1 == count, length, t_row))
        if not last:
            e_row = t_row - c_row
            e_col = jnp.sum(jnp.where(row == lane, e_row, 0.0), axis=1, keepdims=True)
            cross_col = (e_col - jnp.sum(gram * e_row, axis=1, keepdims=True)) * inverse
            cross_row = (e_row - jnp.sum(gram * e_col, axis=0, keepdims=True)) * inverse
            corner = length_sq * inverse * inverse
            gram = jnp.where(row == count, cross_row, jnp.where(lane == count, cross_col, gram))
            gram = jnp.where((row == count) & (lane == count), corner, gram)
        return weights, t_row, inverse, gram

    image_row = known[KEEP + 1:KEEP + 2] * scale
    weights, t_row, inverse0, gram1 = arnoldi(
        assemble(image_row, (ROWS - 1, pick(image_row, KEEP + 1) * scale)), gram, KEEP + 1)
    q21 = assemble(-inverse0 * t_row, (KEEP + 1, scale * inverse0))
    a21 = applied(q21)

    turn = jnp.where(row < KEEP, weights * -inverse0, 0.0)
    chain = jnp.broadcast_to(jnp.sum(
        jnp.where(lane8 == row8 + KEEP - 5, a21, 0.0), axis=1, keepdims=True), (8, LANES))
    sums = [jnp.zeros((8, bz), f32) for _ in range(7)]
    far = []
    for x in range(bx):
        dense = jnp.zeros((by, bz), f32)
        for y in range(by):
            at = x * by + y
            v = (turn[0:8] * t2[x, y, 0:8] + turn[8:16] * t2[x, y, 8:16]
                 + (turn[16:24] * t2[x, y, 16:24] + chain * wrow[at * 8:at * 8 + 8]))
            for shift in (4, 2, 1):
                v = v + pltpu.roll(v, shift, 0)
            for k, part in enumerate(first_block(x, y) + second_block(x, y) + [v]):
                sums[k] = sums[k] + part * v
            dense = jnp.where(row3 == y, v, dense)
        far.append(dense)
    column48 = jnp.sum(jnp.concatenate(sums[0:6], axis=0), axis=1, keepdims=True)
    own = jnp.sum(jnp.where(row48 == lane48, column48, 0.0), axis=0, keepdims=True)
    own = jnp.where(lane1 == 2 * ROWS, jnp.sum(sums[6][0:1], axis=1, keepdims=True), own)
    row_state = reduce_start(2, row_buffers, own)

    back_state = reduce_turn(1, back_buffers, back_state)

    def combine(columns, x, y):
        tiles = first_block(x, y) + second_block(x, y)
        terms = [columns[8 * k:8 * k + 8] * tiles[k] for k in range(6)]
        v = (terms[0] + terms[1]) + (terms[2] + terms[3]) + (terms[4] + terms[5])
        for shift in (4, 2, 1):
            v = v + pltpu.roll(v, shift, 0)
        return v

    def field(columns, x):
        dense = jnp.zeros((by, bz), f32)
        for y in range(by):
            dense = jnp.where(row3 == y, combine(columns, x, y), dense)
        return dense

    def put_field(count, x, value):
        out[count * area + x * by:count * area + (x + 1) * by, :] = value

    q21_col = column(q21)
    for x in range(bx):
        put_field(KEEP, x, w_ref[x] * scale)
        put_field(KEEP + 1, x, field(q21_col, x))

    row_state = reduce_turn(2, row_buffers, row_state)

    tile = reduce_end(back_buffers, back_state)
    def unpack(at):
        top, source, target, width = places[at]
        return jnp.where((lane8 >= source) & (lane8 < source + width),
                         pltpu.roll(tile, (source - target) % LANES, 1), 0.0)
    square = [unpack(3 + k) for k in range(3)]
    diagonal = [jnp.where(lane8 < ROWS + 8 * (k + 1), square[k], 0.0) for k in range(3)]
    second = jnp.concatenate([unpack(6 + k) for k in range(3)], axis=0)
    over = jnp.concatenate([unpack(k) for k in range(3)], axis=0) + jnp.where(
        row < KEEP + 2, second, 0.0)
    strict = jnp.concatenate(
        [over] + [square[k] - diagonal[k] for k in range(3)]
        + [jnp.zeros((LANES - 2 * ROWS, LANES), f32)], axis=0)
    whole = jnp.concatenate(
        [known + jnp.where(row == KEEP + 2, second, 0.0)] + diagonal, axis=0)
    whole = whole + strict[0:2 * ROWS] + strict.T[0:2 * ROWS]

    def products(form_col):
        return jnp.sum(whole * form_col, axis=0, keepdims=True)

    y1 = products(column(a21))
    weights, t_row, inverse1, gram2 = arnoldi(
        assemble(y1, (KEEP + 1, jnp.sum(q21 * y1, axis=1, keepdims=True)),
                 (ROWS - 1, jnp.sum(a21 * y1, axis=1, keepdims=True))), gram1, KEEP + 2)
    t_last = pick(t_row, KEEP + 1)
    t_row = assemble(t_row)
    q22 = inverse1 * (a21 - t_row - t_last * q21)
    near = -inverse1 * (applied(t_row) + t_last * a21)
    q22_col = column(q22)
    near_col = column(near)
    y_near = products(near_col)
    for x in range(bx):
        put_field(KEEP + 2, x, field(q22_col, x))

    own = reduce_end(row_buffers, row_state)
    y2 = jnp.where(lane1 < 2 * ROWS, y_near + inverse1 * own, 0.0)
    inner = jnp.sum(jnp.concatenate([
        q21 * y2, q22 * y2,
        near * (y2 + inverse1 * own)
        + jnp.where(lane1 == 2 * ROWS, inverse1 * inverse1 * own, 0.0),
        jnp.zeros((5, LANES), f32)], axis=0), axis=1, keepdims=True)
    weights, t_row, inverse2, _ = arnoldi(
        assemble(y2, (KEEP + 1, inner[0:1]), (KEEP + 2, inner[1:2]), (ROWS - 1, inner[2:3])),
        gram2, KEEP + 3, True)
    first = jnp.where(row < KEEP, weights, jnp.where(row == KEEP, weights * scale, 0.0))
    last_col = near_col - jnp.concatenate([first, jnp.zeros((ROWS, LANES), f32)], axis=0)
    last_col = last_col - weights[KEEP + 1:KEEP + 2] * q21_col
    last_col = last_col - weights[KEEP + 2:KEEP + 3] * q22_col
    for x in range(bx):
        put_field(KEEP + 3, x, inverse2 * (field(last_col, x) + inverse1 * far[x]))

    for k in range(EXPAND):
        hess[k:k + 1] = hcols[k]
    for copies in (halo_w, halo_r, halo_a, halo_b, halo_t):
        halo_finish(copies)
    for copy in pending:
        copy.wait()


def per_device(krylov_basis, schur_vectors, next_vector, diag_shift, velocity):
    sizes = tuple(lax.axis_size(a) for a in AXES)
    block = next_vector.shape
    bx, by, bz = block
    area = bx * by
    basis = krylov_basis.shape[0]
    cells = float(area * bz * sizes[0] * sizes[1] * sizes[2])
    n0, n1 = sizes[1] * sizes[2], sizes[0]
    f32 = jnp.float32
    vmem = pl.BlockSpec(memory_space=pltpu.VMEM)
    dma = pltpu.SemaphoreType.DMA

    def buffers(rows):
        return [pltpu.VMEM((2, rows, LANES), f32), pltpu.VMEM((n0 - 1, rows, LANES), f32),
                pltpu.VMEM((n1 - 1, rows, LANES), f32)]

    vectors, columns = pl.pallas_call(
        functools.partial(body, sizes, cells),
        out_shape=(
            pltpu.VMEM((ROWS * area, bz), f32),
            pltpu.VMEM((8, LANES), f32),
        ),
        in_specs=[
            pl.BlockSpec(memory_space=pl.ANY) for _ in range(5)
        ],
        out_specs=(vmem, vmem),
        scratch_shapes=[
            pltpu.VMEM(schur_vectors.shape[::-1], f32),
            pltpu.VMEM(block, f32),
            pltpu.VMEM(block, f32),
            pltpu.VMEM((3,) + block, f32),
            pltpu.VMEM((basis * PITCH, bz), f32),
            pltpu.VMEM((7,) + block, f32),
            pltpu.VMEM((bx, by, ROWS, bz), f32),
            pltpu.VMEM((bx, by, ROWS, bz), f32),
            pltpu.VMEM((bx, by, ROWS, bz), f32),
            pltpu.VMEM((area * 8, bz), f32),
            pltpu.VMEM((2,) + block, f32),
            pltpu.VMEM((EXPAND, 2, by, bz), f32),
            pltpu.VMEM((EXPAND, 2) + block, f32),
            pltpu.VMEM((EXPAND, 2) + block, f32),
            pltpu.VMEM((2, 2, by, ROWS, bz), f32),
            pltpu.VMEM((2, 2, bx, ROWS, bz), f32),
            pltpu.VMEM((2, 2, ROWS, bz), f32),
            pltpu.VMEM((2, 2, ROWS, bz), f32),
            pltpu.VMEM((128, area * bz), jnp.bfloat16),
            pltpu.VMEM((144, area * bz), jnp.bfloat16),
            *buffers(3), *buffers(8), *buffers(1),
            dma((5,)), dma((30,)), dma((30,)), dma((6,)), dma((6,)),
        ],
        compiler_params=pltpu.CompilerParams(collective_id=0, has_side_effects=True),
    )(krylov_basis.reshape(basis, area, bz), schur_vectors.T, next_vector, diag_shift, velocity)
    return vectors.reshape((ROWS,) + block), columns[0:EXPAND, 0:ROWS].T


def solution(mesh):
    in_specs = (
        P(None, "gx", "gy", "gz"),
        P(),
        P("gx", "gy", "gz"),
        P("gx", "gy", "gz"),
        P(None, "gx", "gy", "gz"),
    )
    out_specs = (P(None, "gx", "gy", "gz"), P())
    return jax.shard_map(
        per_device, mesh=mesh, in_specs=in_specs, out_specs=out_specs, check_vma=False
    )
```

time: 58.6 us -> 45.9 us (0.78)
  Pallas kernels: 56.5 us -> 43.8 us
    pallas_call x1, Pallas kernels: 56.5 us -> 43.8 us  [per_device(): pl.pallas_call(functools.partial(body, sizes, cells), out_shape=(pltpu.VM...]
where the time goes in v1:
time: 45.9 us; the launch traced here: 45.7 us
  Pallas kernels  43.8 us (95%)
  local copies, waits for them, and re-layouts  1.33 us (3%)
  between operations  0.64 us (1%)
    pallas_call x1, Pallas kernels, per_device(): pl.pallas_call(functools.partial(body, sizes, cells), out_shape=(pltpu.VM...  43.8 us

profile of v1, /device:TPU:1, one launch (start us, length us, event | category | flops | bytes accessed | tf_op | source)
XLA Modules:
  0.0 45.7 jit_solution(4179820168898867400)
XLA Ops:
  0.6 43.8 %shard_map.68 = (f32[768,128]{1,0:T(8,128)S(1)}, f32[8,128]{1,0:T(8,128)S(1)}) custom-call(f32[60,32,128]{2,1,0:T(8,128)} %bitcast.6, f32[20,60]{1,0:T(8,128)} %bitcast.7, f32[4,8,128]{2,1,0:T(8,128)} %w_hbm.1, f32[4,8,128]{2,1,0:T(8,128)} %diag_hbm.1, f32[3,4,8,128]{3,2,1,0:T(8,128)} %vel_hbm.1), custom_call_target="tpu_custom_call" | custom-call | tf_op jit(solution)/shard_map/pallas_call | solution.py:540
  44.4 0.7 %copy.8 = f32[24,4,8,128]{3,2,1,0:T(8,128)} copy(f32[24,4,8,128]{3,2,1,0:T(8,128)S(1)} %bitcast.5) | data formatting | bytes 786432
  45.2 0.6 %slice_bitcast_fusion = f32[24,3]{0,1:T(4,128)} fusion(f32[8,128]{1,0:T(8,128)S(1)} %get-tuple-element.5), kind=kLoop, calls=%fused_computation | loop fusion | bytes 576 | tf_op jit(solution)/shard_map/transpose | solution.py:576

commit v2 on v1

--- a/solution.py
+++ b/solution.py
@@ -13,6 +13,7 @@
 LANES = 128
 UNIT = 16
 PITCH = 40
+SHIFT = 4.0
 AXES = ("gx", "gy", "gz")
 
 
@@ -29,10 +30,22 @@
     schur, w_ref, diag, vel, kry, coef, t0, t1, t2, wrow, image,
     xs, ys, zs, xh, yh, zh, zpack, split0, split1,
     gsend, grecv0, grecv1, bsend, brecv0, brecv1, rsend, rrecv0, rrecv1,
+    isend, irecv0, irecv1,
     load_sem, halo_send, halo_recv, red_send, red_recv,
 ):
     f32, bf16 = jnp.float32, jnp.bfloat16
     place = tuple(lax.axis_index(a) for a in AXES)
+    shifted = [[lax.rem(place[d] + k, sizes[d]) for k in range(sizes[d])] for d in range(3)]
+
+    def partners(phase):
+        return [tuple(shifted[d][step[d]] for d in range(3))
+                for step in partner_steps(phase, sizes)]
+
+    barrier = pltpu.get_barrier_semaphore()
+    for to in partners(0) + partners(1):
+        pl.semaphore_signal(
+            barrier, inc=1, device_id=to, device_id_type=pl.DeviceIdType.MESH)
+
     basis = kry_hbm.shape[0]
     bx, by, bz = w_ref.shape
     area = bx * by
@@ -47,17 +60,6 @@
     for i in range(basis):
         pltpu.make_async_copy(
             kry_hbm.at[i], kry.at[pl.ds(i * PITCH, area)], load_sem.at[1]).start()
-    shifted = [[lax.rem(place[d] + k, sizes[d]) for k in range(sizes[d])] for d in range(3)]
-
-    def partners(phase):
-        return [tuple(shifted[d][step[d]] for d in range(3))
-                for step in partner_steps(phase, sizes)]
-
-    barrier = pltpu.get_barrier_semaphore()
-    for to in partners(0) + partners(1):
-        pl.semaphore_signal(
-            barrier, inc=1, device_id=to, device_id_type=pl.DeviceIdType.MESH)
-
     for d, slots in enumerate(((xs, xh), (ys, yh), (zs, zh))):
         for side in (0, 1):
             def clear(slots=slots, side=side):
@@ -147,6 +149,7 @@
     gram_buffers = (gsend, grecv0, grecv1)
     back_buffers = (bsend, brecv0, brecv1)
     row_buffers = (rsend, rrecv0, rrecv1)
+    image_buffers = (isend, irecv0, irecv1)
 
     lane3 = lax.broadcasted_iota(jnp.int32, (by, bz), 1)
     row3 = lax.broadcasted_iota(jnp.int32, (by, bz), 0)
@@ -224,6 +227,14 @@
 
     dot_nt = functools.partial(
         lax.dot_general, dimension_numbers=(((1,), (1,)), ((), ())), preferred_element_type=f32)
+
+    row = lax.broadcasted_iota(jnp.int32, (ROWS, LANES), 0)
+    lane = lax.broadcasted_iota(jnp.int32, (ROWS, LANES), 1)
+    lane1 = lax.broadcasted_iota(jnp.int32, (1, LANES), 1)
+    row8 = lax.broadcasted_iota(jnp.int32, (8, LANES), 0)
+    lane8 = lax.broadcasted_iota(jnp.int32, (8, LANES), 1)
+    row48 = lax.broadcasted_iota(jnp.int32, (2 * ROWS, LANES), 0)
+    lane48 = lax.broadcasted_iota(jnp.int32, (2 * ROWS, LANES), 1)
 
     halo_w = field_copies(0, w_ref)
     wrow[...] = jnp.zeros_like(wrow)
@@ -262,15 +273,7 @@
             half = 0.5 * vel[d, x]
             coef[2 * d, x] = -1.0 - half
             coef[2 * d + 1, x] = half - 1.0
-        coef[6, x] = 6.0 + diag[x]
-    halo_wait(halo_w)
-    once = field_stencil(w, 0)
-    for x in range(bx):
-        image[0, x] = once[x]
-    halo_a = field_copies(1, image.at[0])
-    halo_start(halo_a)
-    put_row(1, once)
-
+        coef[6, x] = (6.0 - SHIFT) + diag[x]
     zero8 = jnp.zeros((8, 2 * bz), f32)
     for p in range(area // 2):
         put_split(split0, p, jnp.concatenate(both(first_block, p) + [zero8], axis=0))
@@ -278,13 +281,6 @@
     prod = prod[0:24] + prod[32:56] + prod[64:88]
     gram = prod + pltpu.roll(prod, LANES - 32, 1) + pltpu.roll(prod, LANES - 64, 1)
 
-    row = lax.broadcasted_iota(jnp.int32, (ROWS, LANES), 0)
-    lane = lax.broadcasted_iota(jnp.int32, (ROWS, LANES), 1)
-    lane1 = lax.broadcasted_iota(jnp.int32, (1, LANES), 1)
-    row8 = lax.broadcasted_iota(jnp.int32, (8, LANES), 0)
-    lane8 = lax.broadcasted_iota(jnp.int32, (8, LANES), 1)
-    row48 = lax.broadcasted_iota(jnp.int32, (2 * ROWS, LANES), 0)
-    lane48 = lax.broadcasted_iota(jnp.int32, (2 * ROWS, LANES), 1)
     own8 = lane8 // UNIT == row8
 
     def spread(value):
@@ -302,6 +298,26 @@
                 axis=0, keepdims=True)
         for unit in units], axis=0)
     gram_state = reduce_start(0, gram_buffers, packed)
+
+    halo_wait(halo_w)
+    once = field_stencil(w, 0)
+    for x in range(bx):
+        image[0, x] = once[x]
+    sums = [jnp.zeros((8, bz), f32) for _ in range(3)]
+    for x in range(bx):
+        for y in range(by):
+            v = jnp.broadcast_to(once[x][y:y + 1, :], (8, bz))
+            for i, part in enumerate(first_block(x, y)):
+                sums[i] = sums[i] + part * v
+    squares = sum((tile * tile for tile in once[1:]), once[0] * once[0])
+    column24 = jnp.sum(jnp.concatenate(sums, axis=0), axis=1, keepdims=True)
+    own = jnp.sum(jnp.where(row == lane, column24, 0.0), axis=0, keepdims=True)
+    own = jnp.where(lane1 == KEEP + 1, jnp.sum(
+        jnp.sum(squares, axis=0, keepdims=True), axis=1, keepdims=True), own)
+    image_state = reduce_start(3, image_buffers, own)
+    halo_a = field_copies(1, image.at[0])
+    halo_start(halo_a)
+    put_row(1, once)
 
     halo_wait(halo_a)
     twice_w = field_stencil(once, 1)
@@ -334,6 +350,7 @@
                          pltpu.roll(cross[top:top + 8], (target - source) % LANES, 1), tile)
 
     gram_state = reduce_turn(0, gram_buffers, gram_state)
+    image_state = reduce_turn(3, image_buffers, image_state)
     back_state = reduce_start(1, back_buffers, tile)
     for x in range(bx):
         for y in range(by):
@@ -356,13 +373,13 @@
     known = jnp.concatenate(
         [jnp.where(lane8 < 8, units[2], 0.0), units[1], units[0] + corner], axis=0)
     known = known + below.T[0:ROWS]
-    known = jnp.where((lane < KEEP + 2) & (row < KEEP + 2), known, 0.0)
+    known = jnp.where((lane < KEEP + 1) & (row < KEEP + 1), known, 0.0)
     norm_sq = jnp.sum(
         jnp.sum(jnp.where((lane == KEEP) & (row == KEEP), known, 0.0), axis=1, keepdims=True),
         axis=0, keepdims=True)
     scale = 1.0 / jnp.maximum(jnp.sqrt(norm_sq), 0.5)
     gram = known * jnp.where(row == KEEP, scale, 1.0) * jnp.where(lane == KEEP, scale, 1.0)
-    gram = jnp.where((lane < KEEP + 1) & (row < KEEP + 1), gram, 0.0)
+    shifted_row = SHIFT * known[KEEP:KEEP + 1]
 
     def assemble(form, *extra):
         form = jnp.where(lane1 < KEEP, form, jnp.where(lane1 == KEEP, form * scale, 0.0))
@@ -408,15 +425,21 @@
             gram = jnp.where((row == count) & (lane == count), corner, gram)
         return weights, t_row, inverse, gram
 
-    image_row = known[KEEP + 1:KEEP + 2] * scale
+    known_row = reduce_end(image_buffers, image_state)
+    image_sq = jnp.sum(jnp.where(lane1 == KEEP + 1, known_row, jnp.where(
+        lane1 == KEEP, SHIFT * (2.0 * known_row + shifted_row), 0.0)),
+        axis=1, keepdims=True) * (scale * scale)
+    image_row = (known_row + shifted_row) * scale
     weights, t_row, inverse0, gram1 = arnoldi(
-        assemble(image_row, (ROWS - 1, pick(image_row, KEEP + 1) * scale)), gram, KEEP + 1)
-    q21 = assemble(-inverse0 * t_row, (KEEP + 1, scale * inverse0))
-    a21 = applied(q21)
-
-    turn = jnp.where(row < KEEP, weights * -inverse0, 0.0)
-    chain = jnp.broadcast_to(jnp.sum(
-        jnp.where(lane8 == row8 + KEEP - 5, a21, 0.0), axis=1, keepdims=True), (8, LANES))
+        assemble(image_row, (ROWS - 1, image_sq)), gram, KEEP + 1)
+    q21 = assemble(-inverse0 * t_row, (KEEP + 1, scale * inverse0)) + jnp.where(
+        lane1 == KEEP, SHIFT * scale * inverse0, 0.0)
+    b21 = applied(q21)
+    a21 = b21 + SHIFT * q21
+
+    turn = jnp.where(row < KEEP, -weights, 0.0)
+    chain = jnp.where(row8 == 6, (SHIFT - weights[KEEP:KEEP + 1]) * scale,
+                      jnp.where(row8 == 7, scale, 0.0))
     sums = [jnp.zeros((8, bz), f32) for _ in range(7)]
     far = []
     for x in range(bx):
@@ -433,7 +456,8 @@
         far.append(dense)
     column48 = jnp.sum(jnp.concatenate(sums[0:6], axis=0), axis=1, keepdims=True)
     own = jnp.sum(jnp.where(row48 == lane48, column48, 0.0), axis=0, keepdims=True)
-    own = jnp.where(lane1 == 2 * ROWS, jnp.sum(sums[6][0:1], axis=1, keepdims=True), own)
+    own = jnp.where(lane1 == 2 * ROWS, jnp.sum(sums[6][0:1], axis=1, keepdims=True) * inverse0, own)
+    own = own * inverse0
     row_state = reduce_start(2, row_buffers, own)
 
     back_state = reduce_turn(1, back_buffers, back_state)
@@ -475,6 +499,9 @@
     strict = jnp.concatenate(
         [over] + [square[k] - diagonal[k] for k in range(3)]
         + [jnp.zeros((LANES - 2 * ROWS, LANES), f32)], axis=0)
+    known_col = column(known_row, ROWS)
+    known = jnp.where(row == KEEP + 1, jnp.where(lane < KEEP + 2, known_row, 0.0),
+                      jnp.where((lane == KEEP + 1) & (row < KEEP + 1), known_col, known))
     whole = jnp.concatenate(
         [known + jnp.where(row == KEEP + 2, second, 0.0)] + diagonal, axis=0)
     whole = whole + strict[0:2 * ROWS] + strict.T[0:2 * ROWS]
@@ -489,7 +516,7 @@
     t_last = pick(t_row, KEEP + 1)
     t_row = assemble(t_row)
     q22 = inverse1 * (a21 - t_row - t_last * q21)
-    near = -inverse1 * (applied(t_row) + t_last * a21)
+    near = inverse1 * ((SHIFT - t_last) * b21 - applied(t_row)) + SHIFT * q22
     q22_col = column(q22)
     near_col = column(near)
     y_near = products(near_col)
@@ -511,7 +538,7 @@
     last_col = last_col - weights[KEEP + 1:KEEP + 2] * q21_col
     last_col = last_col - weights[KEEP + 2:KEEP + 3] * q22_col
     for x in range(bx):
-        put_field(KEEP + 3, x, inverse2 * (field(last_col, x) + inverse1 * far[x]))
+        put_field(KEEP + 3, x, inverse2 * (field(last_col, x) + inverse1 * inverse0 * far[x]))
 
     for k in range(EXPAND):
         hess[k:k + 1] = hcols[k]
@@ -519,6 +546,16 @@
         halo_finish(copies)
     for copy in pending:
         copy.wait()
+
+
+def place_results(vectors, columns, out, hess, small, sem):
+    large = pltpu.make_async_copy(vectors, out, sem.at[0])
+    large.start()
+    small[...] = columns[0:EXPAND, 0:ROWS]
+    copy = pltpu.make_async_copy(small, hess, sem.at[1])
+    copy.start()
+    copy.wait()
+    large.wait()
 
 
 def per_device(krylov_basis, schur_vectors, next_vector, diag_shift, velocity):
@@ -568,12 +605,23 @@
             pltpu.VMEM((2, 2, ROWS, bz), f32),
             pltpu.VMEM((128, area * bz), jnp.bfloat16),
             pltpu.VMEM((144, area * bz), jnp.bfloat16),
-            *buffers(3), *buffers(8), *buffers(1),
-            dma((5,)), dma((30,)), dma((30,)), dma((6,)), dma((6,)),
+            *buffers(3), *buffers(8), *buffers(1), *buffers(1),
+            dma((5,)), dma((30,)), dma((30,)), dma((8,)), dma((8,)),
         ],
         compiler_params=pltpu.CompilerParams(collective_id=0, has_side_effects=True),
     )(krylov_basis.reshape(basis, area, bz), schur_vectors.T, next_vector, diag_shift, velocity)
-    return vectors.reshape((ROWS,) + block), columns[0:EXPAND, 0:ROWS].T
+    whole = pl.BlockSpec(memory_space=pl.ANY)
+    vectors, columns = pl.pallas_call(
+        place_results,
+        out_shape=(
+            jax.ShapeDtypeStruct((ROWS * area, bz), f32),
+            jax.ShapeDtypeStruct((EXPAND, ROWS), f32),
+        ),
+        in_specs=[vmem, vmem],
+        out_specs=(whole, whole),
+        scratch_shapes=[pltpu.VMEM((EXPAND, ROWS), f32), dma((2,))],
+    )(*(pltpu.with_memory_space_constraint(a, pltpu.VMEM) for a in (vectors, columns)))
+    return vectors.reshape((ROWS,) + block), columns.T
 
 
 def solution(mesh):

time: 45.9 us -> 43.2 us (0.941)
  Pallas kernels: 43.8 us -> 42.4 us
  local copies, waits for them, and re-layouts: 1.33 us -> 0 us
    pallas_call x1, Pallas kernels: 43.8 us -> 41.6 us  [per_device(): pl.pallas_call(functools.partial(body, sizes, cells), out_shape=(pltpu.VM...]
    pallas_call x0 -> x1, Pallas kernels: none -> 0.77 us  [per_device(): pl.pallas_call(place_results, out_shape=(jax.ShapeDtypeStruct((ROWS * are...]
    unnamed x1 -> x0, local copies, waits for them, and re-layouts: 0.75 us -> none
    transpose x1 -> x0, local copies, waits for them, and re-layouts: 0.58 us -> none  [per_device(): return (vectors.reshape((ROWS,) + block), columns[0:EXPAND, 0:ROWS].T)]
where the time goes in v2:
time: 43.2 us; the launch traced here: 43 us
  Pallas kernels  42.4 us (98%)
  between operations  0.64 us (1%)
    pallas_call x1, Pallas kernels, per_device(): pl.pallas_call(functools.partial(body, sizes, cells), out_shape=(pltpu.VM...  41.6 us

profile of v2, /device:TPU:1, one launch (start us, length us, event | category | flops | bytes accessed | tf_op | source)
XLA Modules:
  0.0 43.0 jit_solution(11253795858620373730)
XLA Ops:
  0.6 41.6 %shard_map.68 = (f32[768,128]{1,0:T(8,128)S(1)}, f32[8,128]{1,0:T(8,128)S(1)}) custom-call(f32[60,32,128]{2,1,0:T(8,128)} %bitcast.4, f32[20,60]{1,0:T(8,128)} %bitcast.5, f32[4,8,128]{2,1,0:T(8,128)} %w_hbm.1, f32[4,8,128]{2,1,0:T(8,128)} %diag_hbm.1, f32[3,4,8,128]{3,2,1,0:T(8,128)} %vel_hbm.1), custom_call_target="tpu_custom_call" | custom-call | tf_op jit(solution)/shard_map/pallas_call | solution.py:577
  42.3 0.8 %shard_map.69 = (f32[768,128]{1,0:T(8,128)}, f32[3,24]{1,0:T(4,128)}) custom-call(f32[768,128]{1,0:T(8,128)S(1)} %get-tuple-element.6.vectors, f32[8,128]{1,0:T(8,128)S(1)} %get-tuple-element.7.columns), custom_call_target="tpu_custom_call" | custom-call | tf_op jit(solution)/shard_map/pallas_call | solution.py:614

commit v3 on v2

--- a/solution.py
+++ b/solution.py
@@ -19,8 +19,11 @@
 
 def partner_steps(phase, sizes):
     if phase == 1:
-        return [(dx, 0, 0) for dx in range(1, sizes[0])]
-    return [(0, dy, dz) for dy in range(sizes[1]) for dz in range(sizes[2])][1:]
+        steps = [(dx, 0, 0) for dx in range(1, sizes[0])]
+    else:
+        steps = [(0, dy, dz) for dy in range(sizes[1]) for dz in range(sizes[2])][1:]
+    return sorted(steps, key=lambda step: -sum(
+        min(step[d], sizes[d] - step[d]) for d in range(3)))
 
 
 def body(
@@ -28,9 +31,9 @@
     kry_hbm, schur_hbm, w_hbm, diag_hbm, vel_hbm,
     out, hess,
     schur, w_ref, diag, vel, kry, coef, t0, t1, t2, wrow, image,
-    xs, ys, zs, xh, yh, zh, zpack, split0, split1,
-    gsend, grecv0, grecv1, bsend, brecv0, brecv1, rsend, rrecv0, rrecv1,
-    isend, irecv0, irecv1,
+    xs, ys, zs, zsend, xh, yh, zh, zpack, split0, split1, split2,
+    gsend, grecv0, grecv1, bsend, brecv0, brecv1, isend, irecv0, irecv1,
+    psend, precv, csend, crecv, rsend, rrecv,
     load_sem, halo_send, halo_recv, red_send, red_recv,
 ):
     f32, bf16 = jnp.float32, jnp.bfloat16
@@ -100,7 +103,8 @@
     def field_copies(kind, ref):
         return halo_copies(
             kind,
-            ((ref.at[bx - 1], ref.at[0]), (ref, ref), (ref, ref)),
+            ((ref.at[bx - 1], ref.at[0]), (ref.at[:, by - 1:by], ref.at[:, 0:1]),
+             (zsend.at[kind, 0], zsend.at[kind, 1])),
             tuple((r.at[kind, 0], r.at[kind, 1]) for r in (xs, ys, zs)),
         )
 
@@ -148,7 +152,6 @@
 
     gram_buffers = (gsend, grecv0, grecv1)
     back_buffers = (bsend, brecv0, brecv1)
-    row_buffers = (rsend, rrecv0, rrecv1)
     image_buffers = (isend, irecv0, irecv1)
 
     lane3 = lax.broadcasted_iota(jnp.int32, (by, bz), 1)
@@ -161,10 +164,10 @@
             here = v[x]
             xb = v[x - 1] if x > 0 else xs[kind, 0]
             xa = v[x + 1] if x < bx - 1 else xs[kind, 1]
-            yb = jnp.where(row3 == 0, ys[kind, 0, x, by - 1:by, :], pltpu.roll(here, 1, 0))
-            ya = jnp.where(row3 == by - 1, ys[kind, 1, x, 0:1, :], pltpu.roll(here, by - 1, 0))
-            zb = jnp.where(lane3 == 0, zs[kind, 0, x, :, bz - 1:bz], pltpu.roll(here, 1, 1))
-            za = jnp.where(lane3 == bz - 1, zs[kind, 1, x, :, 0:1], pltpu.roll(here, bz - 1, 1))
+            yb = jnp.where(row3 == 0, ys[kind, 0, x], pltpu.roll(here, 1, 0))
+            ya = jnp.where(row3 == by - 1, ys[kind, 1, x], pltpu.roll(here, by - 1, 0))
+            zb = jnp.where(lane3 == 0, zs[kind, 0, :, x:x + 1], pltpu.roll(here, 1, 1))
+            za = jnp.where(lane3 == bz - 1, zs[kind, 1, :, x:x + 1], pltpu.roll(here, bz - 1, 1))
             res.append(coef[6, x] * here + (coef[0, x] * xb + coef[1, x] * xa)
                        + (coef[2, x] * yb + coef[3, x] * ya)
                        + (coef[4, x] * zb + coef[5, x] * za))
@@ -188,6 +191,13 @@
                 target[x, y] = (c[6] * here + (c[0] * xb + c[1] * xa)
                                 + (c[2] * yb + c[3] * ya) + (c[4] * zb + c[5] * za))
 
+    def pack_ends(kind, tiles):
+        for side, edge in enumerate((bz - 1, 0)):
+            face = tiles[0] if edge == 0 else pltpu.roll(tiles[0], 1, 1)
+            for x in range(1, bx):
+                face = jnp.where(lane3 == x, pltpu.roll(tiles[x], (x - edge) % bz, 1), face)
+            zsend[kind, side] = face
+
     def pack_faces(level, source):
         for side, edge in enumerate((bz - 1, 0)):
             face = jnp.zeros((ROWS, bz), f32)
@@ -211,15 +221,34 @@
     def second_block(x, y):
         return [t1[x, y, 0:8], t1[x, y, 8:16], t1[x, y, 16:24]]
 
-    def put_split(ref, p, u):
+    def third_block(x, y):
+        return [t2[x, y, 0:8], t2[x, y, 8:16], t2[x, y, 16:24]]
+
+    def row_dots(tiles, *blocks):
+        sums = [jnp.zeros((8, bz), f32) for _ in range(3 * len(blocks))]
+        for x in range(bx):
+            for y in range(by):
+                v = jnp.broadcast_to(tiles[x][y:y + 1, :], (8, bz))
+                for k, part in enumerate([t for block in blocks for t in block(x, y)]):
+                    sums[k] = sums[k] + part * v
+        return [jnp.sum(total, axis=1, keepdims=True) for total in sums]
+
+    def as_row(columns):
+        count = 8 * len(columns)
+        own = (lax.broadcasted_iota(jnp.int32, (count, LANES), 0)
+               == lax.broadcasted_iota(jnp.int32, (count, LANES), 1))
+        return jnp.sum(jnp.where(own, jnp.concatenate(columns, axis=0), 0.0), axis=0, keepdims=True)
+
+    def put_split(ref, p, u, first=0, pitch=None):
         n = u.shape[0]
+        pitch = pitch or n
         at = pl.ds(p * 2 * bz, 2 * bz)
         high = u.astype(bf16)
         rest = u - high.astype(f32)
         mid = rest.astype(bf16)
-        ref[0:n, at] = high
-        ref[n:2 * n, at] = mid
-        ref[2 * n:3 * n, at] = (rest - mid.astype(f32)).astype(bf16)
+        ref[first:first + n, at] = high
+        ref[first + pitch:first + pitch + n, at] = mid
+        ref[first + 2 * pitch:first + 2 * pitch + n, at] = (rest - mid.astype(f32)).astype(bf16)
 
     def both(block, p):
         return [jnp.concatenate([block(*divmod(2 * p, by))[k], block(*divmod(2 * p + 1, by))[k]],
@@ -240,11 +269,7 @@
     wrow[...] = jnp.zeros_like(wrow)
     t0[:, :, 16:24] = jnp.zeros((bx, by, 8, bz), f32)
     split0[96:128] = jnp.zeros((32, split0.shape[1]), bf16)
-    loads[0].wait()
-    pl.semaphore_wait(barrier, len(partners(0)) + len(partners(1)))
-    halo_start(halo_w)
-    w = [w_ref[x] for x in range(bx)]
-    put_row(0, w)
+    split2[96:128] = jnp.zeros((32, split2.shape[1]), bf16)
 
     loads[2].wait()
     loads[1].wait()
@@ -264,6 +289,12 @@
             t0[x, y, 0:KEEP] = r[:, k * bz:(k + 1) * bz]
     pack_faces(0, t0)
     halo_r = rows_copies(0, t0)
+    loads[0].wait()
+    w = [w_ref[x] for x in range(bx)]
+    pack_ends(0, w)
+    put_row(0, w)
+    pl.semaphore_wait(barrier, len(partners(0)) + len(partners(1)))
+    halo_start(halo_w)
     halo_start(halo_r)
 
     loads[3].wait()
@@ -303,15 +334,9 @@
     once = field_stencil(w, 0)
     for x in range(bx):
         image[0, x] = once[x]
-    sums = [jnp.zeros((8, bz), f32) for _ in range(3)]
-    for x in range(bx):
-        for y in range(by):
-            v = jnp.broadcast_to(once[x][y:y + 1, :], (8, bz))
-            for i, part in enumerate(first_block(x, y)):
-                sums[i] = sums[i] + part * v
+    pack_ends(1, once)
+    own = as_row(row_dots(once, first_block))
     squares = sum((tile * tile for tile in once[1:]), once[0] * once[0])
-    column24 = jnp.sum(jnp.concatenate(sums, axis=0), axis=1, keepdims=True)
-    own = jnp.sum(jnp.where(row == lane, column24, 0.0), axis=0, keepdims=True)
     own = jnp.where(lane1 == KEEP + 1, jnp.sum(
         jnp.sum(squares, axis=0, keepdims=True), axis=1, keepdims=True), own)
     image_state = reduce_start(3, image_buffers, own)
@@ -319,13 +344,6 @@
     halo_start(halo_a)
     put_row(1, once)
 
-    halo_wait(halo_a)
-    twice_w = field_stencil(once, 1)
-    for x in range(bx):
-        image[1, x] = twice_w[x]
-    halo_b = field_copies(2, image.at[1])
-    halo_start(halo_b)
-    put_row(2, twice_w)
     halo_wait(halo_r)
     rows_stencil(0, t0, t1)
     pack_faces(1, t1)
@@ -342,23 +360,82 @@
     cross = left + pltpu.roll(left, LANES - 48, 1) + jnp.where(
         lane48 < 32, pltpu.roll(left, LANES - 96, 1), pltpu.roll(right, 32, 1))
 
+    halo_wait(halo_a)
+    twice_w = field_stencil(once, 1)
+    for x in range(bx):
+        image[1, x] = twice_w[x]
+    pack_ends(2, twice_w)
+    halo_b = field_copies(2, image.at[1])
+    halo_start(halo_b)
+    put_row(2, twice_w)
+
     places = ((0, 24, 0, 24), (8, 24, 24, 24), (16, 24, 48, 24), (24, 24, 72, 24),
-              (32, 32, 96, 16), (40, 40, 112, 8), (0, 22, 120, 1), (8, 22, 121, 1), (16, 22, 122, 1))
+              (32, 32, 96, 16), (40, 40, 112, 8))
     tile = jnp.zeros((8, LANES), f32)
     for top, source, target, width in places:
         tile = jnp.where((lane8 >= target) & (lane8 < target + width),
                          pltpu.roll(cross[top:top + 8], (target - source) % LANES, 1), tile)
+    for k, col in enumerate(row_dots(twice_w, first_block, second_block)):
+        tile = jnp.where(lane8 == 120 + k, col, tile)
+    back_state = reduce_start(1, back_buffers, tile)
+    for p in range(area // 2):
+        put_split(split1, p, jnp.concatenate(
+            both(first_block, p)[2:3] + both(second_block, p)[0:1], axis=0), 16, 2 * ROWS)
+
+    halo_wait(halo_t)
+    rows_stencil(1, t1, t2)
+    def third_tail(x, y):
+        return third_block(x, y)[0:2] + [t2[x, y, 16:24]
+                                         + wrow[(x * by + y) * 8:(x * by + y) * 8 + 8]]
+    for p in range(area // 2):
+        put_split(split2, p, jnp.concatenate(both(third_tail, p) + [zero8], axis=0))
+
+    def fold(prod):
+        return prod + pltpu.roll(prod, LANES - 32, 1) + pltpu.roll(prod, LANES - 64, 1)
+
+    prod = dot_nt(split1[...], split2[...])
+    mixed = fold(prod[0:48] + prod[48:96] + prod[96:144])
+    prod = dot_nt(split2[0:96], split2[...])
+    square = fold(prod[0:24] + prod[32:56] + prod[64:88])
+
+    def pack_mixed(value):
+        tile = jnp.zeros((8, LANES), f32)
+        for k in range(5):
+            tile = jnp.where((lane8 >= ROWS * k) & (lane8 < ROWS * k + ROWS),
+                             pltpu.roll(value[8 * k:8 * k + 8], ROWS * k, 1), tile)
+        return tile
+
+    def pack_square(last, value):
+        tile = jnp.where(lane8 < ROWS, last, 0.0)
+        start = ROWS
+        for k in range(3):
+            width = ROWS - 8 * k
+            for half in (0, 1):
+                part = value[8 * k:8 * k + 8]
+                if half:
+                    part = pltpu.roll(part, 4, 0)
+                tile = jnp.where((lane8 >= start) & (lane8 < start + width),
+                                 pltpu.roll(part, (start - 8 * k) % LANES, 1), tile)
+                start = start + width
+        return tile
 
     gram_state = reduce_turn(0, gram_buffers, gram_state)
     image_state = reduce_turn(3, image_buffers, image_state)
-    back_state = reduce_start(1, back_buffers, tile)
+    tile = pack_mixed(mixed)
+    psend[0] = tile[0:4]
+    psend[1] = tile[4:8]
+    psend[2] = pack_square(mixed[40:48], square)[0:4]
+    mixed_arrival = exchange(2, psend, precv, 1)
+
+    halo_wait(halo_b)
+    thrice_w = field_stencil(twice_w, 2)
+    put_row(3, thrice_w)
+    csend[...] = as_row(row_dots(thrice_w, first_block, second_block, third_block))
+    chain_arrival = exchange(4, csend, crecv, 1)
     for x in range(bx):
         for y in range(by):
             out[pl.ds(x * by + y, ROWS, stride=area), :] = t0[x, y]
-    halo_wait(halo_b)
-    put_row(3, field_stencil(twice_w, 2))
-    halo_wait(halo_t)
-    rows_stencil(1, t1, t2)
+    back_state = reduce_turn(1, back_buffers, back_state)
 
     packed = reduce_end(gram_buffers, gram_state)
     units = [
@@ -437,10 +514,37 @@
     b21 = applied(q21)
     a21 = b21 + SHIFT * q21
 
+    q_square = jnp.where(lane1 < KEEP, q21, 0.0) + jnp.where(
+        lane1 == KEEP + 2, pltpu.roll(q21, 2, 1), 0.0)
+    q_last = pick(q21, KEEP + 1)
+    spread_q = jnp.broadcast_to(q_square, (2 * ROWS, LANES))
+    pairs = column(q_square, ROWS) * q_square * jnp.where(lane < row // 8 * 8 + 8, 1.0, 2.0)
+    weigh_mixed = pack_mixed(spread_q)
+    weigh_square = pack_square(spread_q[0:8], pairs)[0:4]
+    weigh_chain = q_last * (2.0 * pltpu.roll(jnp.where(lane1 < KEEP, q21, 0.0), 2 * ROWS, 1)
+                            + jnp.where(lane1 == KEEP + 2, 2.0 * q_square, 0.0)
+                            + jnp.where(lane1 == KEEP + 3, q_last, 0.0))
+    chain_row = gather_sum(chain_arrival, csend[...], crecv)
+    chain_sq = jnp.sum(chain_row * weigh_chain, axis=1, keepdims=True)
+    total = gather_sum(mixed_arrival, psend[...], precv)
+    tile = jnp.concatenate([total[0], total[1]], axis=0) * weigh_mixed
+    last = total[2] * weigh_square
+    lane4 = lax.broadcasted_iota(jnp.int32, (4, LANES), 1)
+    columns = [jnp.sum(jnp.where((lane8 >= ROWS * k) & (lane8 < ROWS * k + ROWS), tile, 0.0),
+                       axis=1, keepdims=True) for k in range(5)]
+    columns.append(jnp.concatenate([
+        jnp.sum(jnp.where(lane4 < ROWS, last, 0.0), axis=1, keepdims=True),
+        jnp.zeros((4, 1), f32)], axis=0))
+    far_sq = chain_sq + jnp.sum(jnp.sum(
+        jnp.where(lane4 < ROWS, 0.0, last), axis=0, keepdims=True), axis=1, keepdims=True)
+    own = jnp.where(lane1 < 2 * ROWS, as_row(columns) + q_last * chain_row, 0.0)
+    own = jnp.where(lane1 == 2 * ROWS, far_sq, own)
+    rsend[...] = own
+    row_state = own, exchange(2, rsend, rrecv, 0)
+
     turn = jnp.where(row < KEEP, -weights, 0.0)
     chain = jnp.where(row8 == 6, (SHIFT - weights[KEEP:KEEP + 1]) * scale,
                       jnp.where(row8 == 7, scale, 0.0))
-    sums = [jnp.zeros((8, bz), f32) for _ in range(7)]
     far = []
     for x in range(bx):
         dense = jnp.zeros((by, bz), f32)
@@ -450,17 +554,8 @@
                  + (turn[16:24] * t2[x, y, 16:24] + chain * wrow[at * 8:at * 8 + 8]))
             for shift in (4, 2, 1):
                 v = v + pltpu.roll(v, shift, 0)
-            for k, part in enumerate(first_block(x, y) + second_block(x, y) + [v]):
-                sums[k] = sums[k] + part * v
             dense = jnp.where(row3 == y, v, dense)
         far.append(dense)
-    column48 = jnp.sum(jnp.concatenate(sums[0:6], axis=0), axis=1, keepdims=True)
-    own = jnp.sum(jnp.where(row48 == lane48, column48, 0.0), axis=0, keepdims=True)
-    own = jnp.where(lane1 == 2 * ROWS, jnp.sum(sums[6][0:1], axis=1, keepdims=True) * inverse0, own)
-    own = own * inverse0
-    row_state = reduce_start(2, row_buffers, own)
-
-    back_state = reduce_turn(1, back_buffers, back_state)
 
     def combine(columns, x, y):
         tiles = first_block(x, y) + second_block(x, y)
@@ -484,8 +579,6 @@
         put_field(KEEP, x, w_ref[x] * scale)
         put_field(KEEP + 1, x, field(q21_col, x))
 
-    row_state = reduce_turn(2, row_buffers, row_state)
-
     tile = reduce_end(back_buffers, back_state)
     def unpack(at):
         top, source, target, width = places[at]
@@ -493,11 +586,13 @@
                          pltpu.roll(tile, (source - target) % LANES, 1), 0.0)
     square = [unpack(3 + k) for k in range(3)]
     diagonal = [jnp.where(lane8 < ROWS + 8 * (k + 1), square[k], 0.0) for k in range(3)]
-    second = jnp.concatenate([unpack(6 + k) for k in range(3)], axis=0)
+    columns = [jnp.where(lane8 == KEEP + 2, pltpu.roll(tile, (KEEP + 2 - 120 - k) % LANES, 1), 0.0)
+               for k in range(6)]
+    second = jnp.concatenate(columns[0:3], axis=0)
     over = jnp.concatenate([unpack(k) for k in range(3)], axis=0) + jnp.where(
         row < KEEP + 2, second, 0.0)
     strict = jnp.concatenate(
-        [over] + [square[k] - diagonal[k] for k in range(3)]
+        [over] + [square[k] - diagonal[k] + columns[3 + k] for k in range(3)]
         + [jnp.zeros((LANES - 2 * ROWS, LANES), f32)], axis=0)
     known_col = column(known_row, ROWS)
     known = jnp.where(row == KEEP + 1, jnp.where(lane < KEEP + 2, known_row, 0.0),
@@ -523,7 +618,12 @@
     for x in range(bx):
         put_field(KEEP + 2, x, field(q22_col, x))
 
-    own = reduce_end(row_buffers, row_state)
+    for copies in (halo_w, halo_r, halo_a, halo_b, halo_t):
+        halo_finish(copies)
+    for copy in pending[:-1]:
+        copy.wait()
+
+    own = gather_sum(row_state[1], row_state[0], rrecv) * (1.0 / cells)
     y2 = jnp.where(lane1 < 2 * ROWS, y_near + inverse1 * own, 0.0)
     inner = jnp.sum(jnp.concatenate([
         q21 * y2, q22 * y2,
@@ -542,10 +642,7 @@
 
     for k in range(EXPAND):
         hess[k:k + 1] = hcols[k]
-    for copies in (halo_w, halo_r, halo_a, halo_b, halo_t):
-        halo_finish(copies)
-    for copy in pending:
-        copy.wait()
+    pending[-1].wait()
 
 
 def place_results(vectors, columns, out, hess, small, sem):
@@ -597,16 +694,21 @@
             pltpu.VMEM((area * 8, bz), f32),
             pltpu.VMEM((2,) + block, f32),
             pltpu.VMEM((EXPAND, 2, by, bz), f32),
-            pltpu.VMEM((EXPAND, 2) + block, f32),
-            pltpu.VMEM((EXPAND, 2) + block, f32),
+            pltpu.VMEM((EXPAND, 2, bx, 1, bz), f32),
+            pltpu.VMEM((EXPAND, 2, by, bz), f32),
+            pltpu.VMEM((EXPAND, 2, by, bz), f32),
             pltpu.VMEM((2, 2, by, ROWS, bz), f32),
             pltpu.VMEM((2, 2, bx, ROWS, bz), f32),
             pltpu.VMEM((2, 2, ROWS, bz), f32),
             pltpu.VMEM((2, 2, ROWS, bz), f32),
             pltpu.VMEM((128, area * bz), jnp.bfloat16),
             pltpu.VMEM((144, area * bz), jnp.bfloat16),
-            *buffers(3), *buffers(8), *buffers(1), *buffers(1),
-            dma((5,)), dma((30,)), dma((30,)), dma((8,)), dma((8,)),
+            pltpu.VMEM((128, area * bz), jnp.bfloat16),
+            *buffers(3), *buffers(8), *buffers(1),
+            pltpu.VMEM((3, 4, LANES), f32), pltpu.VMEM((n1 - 1, 3, 4, LANES), f32),
+            pltpu.VMEM((1, LANES), f32), pltpu.VMEM((n1 - 1, 1, LANES), f32),
+            pltpu.VMEM((1, LANES), f32), pltpu.VMEM((n0 - 1, 1, LANES), f32),
+            dma((5,)), dma((30,)), dma((30,)), dma((10,)), dma((10,)),
         ],
         compiler_params=pltpu.CompilerParams(collective_id=0, has_side_effects=True),
     )(krylov_basis.reshape(basis, area, bz), schur_vectors.T, next_vector, diag_shift, velocity)

time: 43.2 us -> 39.2 us (0.907)
  Pallas kernels: 42.4 us -> 38.3 us
    pallas_call x1, Pallas kernels: 41.6 us -> 37.6 us  [per_device(): pl.pallas_call(functools.partial(body, sizes, cells), out_shape=(pltpu.VM...]
where the time goes in v3:
time: 39.2 us; the launch traced here: 39 us
  Pallas kernels  38.3 us (98%)
  between operations  0.64 us (2%)
    pallas_call x1, Pallas kernels, per_device(): pl.pallas_call(functools.partial(body, sizes, cells), out_shape=(pltpu.VM...  37.6 us

profile of v3, /device:TPU:1, one launch (start us, length us, event | category | flops | bytes accessed | tf_op | source)
XLA Modules:
  0.0 39.0 jit_solution(17411036080825657972)
XLA Ops:
  0.6 37.6 %shard_map.68 = (f32[768,128]{1,0:T(8,128)S(1)}, f32[8,128]{1,0:T(8,128)S(1)}) custom-call(f32[60,32,128]{2,1,0:T(8,128)} %bitcast.4, f32[20,60]{1,0:T(8,128)} %bitcast.5, f32[4,8,128]{2,1,0:T(8,128)} %w_hbm.1, f32[4,8,128]{2,1,0:T(8,128)} %diag_hbm.1, f32[3,4,8,128]{3,2,1,0:T(8,128)} %vel_hbm.1), custom_call_target="tpu_custom_call" | custom-call | tf_op jit(solution)/shard_map/pallas_call | solution.py:674
  38.2 0.8 %shard_map.69 = (f32[768,128]{1,0:T(8,128)}, f32[3,24]{1,0:T(4,128)}) custom-call(f32[768,128]{1,0:T(8,128)S(1)} %get-tuple-element.6.vectors, f32[8,128]{1,0:T(8,128)S(1)} %get-tuple-element.7.columns), custom_call_target="tpu_custom_call" | custom-call | tf_op jit(solution)/shard_map/pallas_call | solution.py:716

commit v4 on v3

--- a/solution.py
+++ b/solution.py
@@ -31,9 +31,8 @@
     kry_hbm, schur_hbm, w_hbm, diag_hbm, vel_hbm,
     out, hess,
     schur, w_ref, diag, vel, kry, coef, t0, t1, t2, wrow, image,
-    xs, ys, zs, zsend, xh, yh, zh, zpack, split0, split1, split2,
-    gsend, grecv0, grecv1, bsend, brecv0, brecv1, isend, irecv0, irecv1,
-    psend, precv, csend, crecv, rsend, rrecv,
+    hw, hr, faces, zpack, split0, split1, split2,
+    gsend, gslots, bsend, bslots, psend, precv, isend, csend, rsend, rslots,
     load_sem, halo_send, halo_recv, red_send, red_recv,
 ):
     f32, bf16 = jnp.float32, jnp.bfloat16
@@ -63,70 +62,51 @@
     for i in range(basis):
         pltpu.make_async_copy(
             kry_hbm.at[i], kry.at[pl.ds(i * PITCH, area)], load_sem.at[1]).start()
-    for d, slots in enumerate(((xs, xh), (ys, yh), (zs, zh))):
-        for side in (0, 1):
-            def clear(slots=slots, side=side):
-                for ref in slots:
-                    for k in range(ref.shape[0]):
-                        ref[k, side] = jnp.zeros(ref.shape[2:], f32)
-            pl.when(place[d] == (0 if side == 0 else sizes[d] - 1))(clear)
-
-    def halo_copies(kind, sources, targets):
+    def halo_copies(sources, targets, send, recv):
         found = []
         for d in range(3):
             for side in (0, 1):
-                at = (kind * 3 + d) * 2 + side
                 to = list(place)
-                to[d] = place[d] + (1 if side == 0 else -1)
-                can_send = place[d] < sizes[d] - 1 if side == 0 else place[d] > 0
-                can_recv = place[d] > 0 if side == 0 else place[d] < sizes[d] - 1
-                found.append((
-                    pltpu.make_async_remote_copy(
-                        src_ref=sources[d][side], dst_ref=targets[d][side],
-                        send_sem=halo_send.at[at], recv_sem=halo_recv.at[at],
-                        device_id=tuple(to), device_id_type=pl.DeviceIdType.MESH,
-                    ), can_send, can_recv))
+                to[d] = shifted[d][1 if side == 0 else sizes[d] - 1]
+                found.append(pltpu.make_async_remote_copy(
+                    src_ref=sources[d][side], dst_ref=targets[d][side],
+                    send_sem=halo_send.at[send], recv_sem=halo_recv.at[recv],
+                    device_id=tuple(to), device_id_type=pl.DeviceIdType.MESH,
+                ))
         return found
 
     def halo_start(copies):
-        for copy, can_send, _ in copies:
-            pl.when(can_send)(copy.start)
-
-    def halo_wait(copies):
-        for copy, _, can_recv in copies:
-            pl.when(can_recv)(copy.wait_recv)
-
-    def halo_finish(copies):
-        for copy, can_send, _ in copies:
-            pl.when(can_send)(copy.wait_send)
+        for copy in copies:
+            copy.start()
+
+    def field_wait(kind):
+        pltpu.make_async_copy(hw.at[kind], hw.at[kind], halo_recv.at[kind]).wait()
+
+    def rows_wait(level):
+        landed = hr.at[level, :, :, 0:KEEP]
+        pltpu.make_async_copy(landed, landed, halo_recv.at[EXPAND + level]).wait()
 
     def field_copies(kind, ref):
         return halo_copies(
-            kind,
-            ((ref.at[bx - 1], ref.at[0]), (ref.at[:, by - 1:by], ref.at[:, 0:1]),
-             (zsend.at[kind, 0], zsend.at[kind, 1])),
-            tuple((r.at[kind, 0], r.at[kind, 1]) for r in (xs, ys, zs)),
-        )
+            ((ref.at[bx - 1], ref.at[0]), (faces.at[kind, 0, 0], faces.at[kind, 1, 0]),
+             (faces.at[kind, 0, 1], faces.at[kind, 1, 1])),
+            tuple((hw.at[kind, 0, d], hw.at[kind, 1, d]) for d in range(3)), 0, kind)
 
     def rows_copies(level, ref):
         return halo_copies(
-            EXPAND + level,
-            ((ref.at[bx - 1], ref.at[0]), (ref.at[:, by - 1], ref.at[:, 0]),
-             (zpack.at[level, 0], zpack.at[level, 1])),
-            tuple((r.at[level, 0], r.at[level, 1]) for r in (xh, yh, zh)),
-        )
-
-    pending = []
-
-    def exchange(kind, send, slots, phase):
-        at = kind * 2 + phase
+            ((ref.at[bx - 1, :, 0:KEEP], ref.at[0, :, 0:KEEP]),
+             (ref.at[:, by - 1, 0:KEEP], ref.at[:, 0, 0:KEEP]),
+             (zpack.at[level, 0, 0:KEEP], zpack.at[level, 1, 0:KEEP])),
+            tuple((hr.at[level, 0, part, 0:KEEP], hr.at[level, 1, part, 0:KEEP])
+                  for part in (pl.ds(0, by), pl.ds(by, bx), by + bx)), 1, EXPAND + level)
+
+    def exchange(kind, at, send, slots, phase):
         for k, to in enumerate(partners(phase)):
             pltpu.make_async_remote_copy(
-                src_ref=send, dst_ref=slots.at[k], send_sem=red_send.at[at],
+                src_ref=send, dst_ref=slots.at[k], send_sem=red_send.at[kind],
                 recv_sem=red_recv.at[at],
                 device_id=to, device_id_type=pl.DeviceIdType.MESH,
             ).start()
-        pending.append(pltpu.make_async_copy(slots, slots, red_send.at[at]))
         return pltpu.make_async_copy(slots, slots, red_recv.at[at])
 
     def gather_sum(arrival, own, slots):
@@ -136,23 +116,26 @@
             terms = [sum(terms[k + 1:k + 2], terms[k]) for k in range(0, len(terms), 2)]
         return terms[0]
 
-    def reduce_start(kind, buffers, value):
-        send, slots0, _ = buffers
+    def reduce_start(buffers, value):
+        kind, at, send, slots0, _ = buffers
         send[0] = value
-        return value, exchange(kind, send.at[0], slots0, 0)
-
-    def reduce_turn(kind, buffers, state):
-        send, slots0, slots1 = buffers
+        return value, exchange(kind, at, send.at[0], slots0, 0)
+
+    def reduce_turn(buffers, state):
+        kind, at, send, slots0, slots1 = buffers
         value = gather_sum(state[1], state[0], slots0)
         send[1] = value
-        return value, exchange(kind, send.at[1], slots1, 1)
+        return value, exchange(kind, at + 1, send.at[1], slots1, 1)
 
     def reduce_end(buffers, state):
-        return gather_sum(state[1], state[0], buffers[2]) * (1.0 / cells)
-
-    gram_buffers = (gsend, grecv0, grecv1)
-    back_buffers = (bsend, brecv0, brecv1)
-    image_buffers = (isend, irecv0, irecv1)
+        return gather_sum(state[1], state[0], buffers[4]) * (1.0 / cells)
+
+    n0, n1 = len(partner_steps(0, sizes)), len(partner_steps(1, sizes))
+    gram_buffers = (0, 0, gsend, gslots.at[pl.ds(0, n0)], gslots.at[pl.ds(n0, n1)])
+    back_buffers = (1, 2, bsend, bslots.at[pl.ds(0, n0)], bslots.at[pl.ds(n0, n1)])
+    image_buffers = (3, 4, isend, rslots.at[pl.ds(0, n0)], rslots.at[pl.ds(n0, n1)])
+    crecv = rslots.at[pl.ds(n0 + n1, n1)]
+    rrecv = rslots.at[pl.ds(n0 + 2 * n1, n0)]
 
     lane3 = lax.broadcasted_iota(jnp.int32, (by, bz), 1)
     row3 = lax.broadcasted_iota(jnp.int32, (by, bz), 0)
@@ -162,41 +145,46 @@
         res = []
         for x in range(bx):
             here = v[x]
-            xb = v[x - 1] if x > 0 else xs[kind, 0]
-            xa = v[x + 1] if x < bx - 1 else xs[kind, 1]
-            yb = jnp.where(row3 == 0, ys[kind, 0, x], pltpu.roll(here, 1, 0))
-            ya = jnp.where(row3 == by - 1, ys[kind, 1, x], pltpu.roll(here, by - 1, 0))
-            zb = jnp.where(lane3 == 0, zs[kind, 0, :, x:x + 1], pltpu.roll(here, 1, 1))
-            za = jnp.where(lane3 == bz - 1, zs[kind, 1, :, x:x + 1], pltpu.roll(here, bz - 1, 1))
+            xb = v[x - 1] if x > 0 else hw[kind, 0, 0]
+            xa = v[x + 1] if x < bx - 1 else hw[kind, 1, 0]
+            yb = jnp.where(row3 == 0, hw[kind, 0, 1, x:x + 1, :], pltpu.roll(here, 1, 0))
+            ya = jnp.where(row3 == by - 1, hw[kind, 1, 1, x:x + 1, :], pltpu.roll(here, by - 1, 0))
+            zb = jnp.where(lane3 == 0, hw[kind, 0, 2, :, x:x + 1], pltpu.roll(here, 1, 1))
+            za = jnp.where(lane3 == bz - 1, hw[kind, 1, 2, :, x:x + 1], pltpu.roll(here, bz - 1, 1))
             res.append(coef[6, x] * here + (coef[0, x] * xb + coef[1, x] * xa)
                        + (coef[2, x] * yb + coef[3, x] * ya)
                        + (coef[4, x] * zb + coef[5, x] * za))
         return res
 
-    def rows_stencil(level, source, target):
-        low, high = zh[level, 0], zh[level, 1]
-        for x in range(bx):
-            for y in range(by):
-                at = x * by + y
-                here = source[x, y]
-                xb = source[x - 1, y] if x > 0 else xh[level, 0, y]
-                xa = source[x + 1, y] if x < bx - 1 else xh[level, 1, y]
-                yb = source[x, y - 1] if y > 0 else yh[level, 0, x]
-                ya = source[x, y + 1] if y < by - 1 else yh[level, 1, x]
-                zb = jnp.where(lane24 == 0, pltpu.roll(low, (bz - at) % bz, 1),
-                               pltpu.roll(here, 1, 1))
-                za = jnp.where(lane24 == bz - 1, pltpu.roll(high, bz - 1 - at, 1),
-                               pltpu.roll(here, bz - 1, 1))
-                c = [coef[k, x, y:y + 1, :] for k in range(7)]
-                target[x, y] = (c[6] * here + (c[0] * xb + c[1] * xa)
-                                + (c[2] * yb + c[3] * ya) + (c[4] * zb + c[5] * za))
+    inner = [(x, y) for x in range(1, bx - 1) for y in range(1, by - 1)]
+    outer = [(x, y) for x in range(bx) for y in range(by) if (x, y) not in inner]
+
+    def rows_stencil(level, source, target, where):
+        low, high = hr[level, 0, by + bx], hr[level, 1, by + bx]
+        for x, y in where:
+            at = x * by + y
+            here = source[x, y]
+            xb = source[x - 1, y] if x > 0 else hr[level, 0, y]
+            xa = source[x + 1, y] if x < bx - 1 else hr[level, 1, y]
+            yb = source[x, y - 1] if y > 0 else hr[level, 0, by + x]
+            ya = source[x, y + 1] if y < by - 1 else hr[level, 1, by + x]
+            zb = jnp.where(lane24 == 0, pltpu.roll(low, (bz - at) % bz, 1),
+                           pltpu.roll(here, 1, 1))
+            za = jnp.where(lane24 == bz - 1, pltpu.roll(high, bz - 1 - at, 1),
+                           pltpu.roll(here, bz - 1, 1))
+            c = [coef[k, x, y:y + 1, :] for k in range(7)]
+            target[x, y] = (c[6] * here + (c[0] * xb + c[1] * xa)
+                            + (c[2] * yb + c[3] * ya) + (c[4] * zb + c[5] * za))
 
     def pack_ends(kind, tiles):
-        for side, edge in enumerate((bz - 1, 0)):
-            face = tiles[0] if edge == 0 else pltpu.roll(tiles[0], 1, 1)
-            for x in range(1, bx):
-                face = jnp.where(lane3 == x, pltpu.roll(tiles[x], (x - edge) % bz, 1), face)
-            zsend[kind, side] = face
+        for side, (near, edge) in enumerate(((by - 1, bz - 1), (0, 0))):
+            rows = jnp.zeros((by, bz), f32)
+            lanes = jnp.zeros((by, bz), f32)
+            for x in range(bx):
+                rows = jnp.where(row3 == x, pltpu.roll(tiles[x], (x - near) % by, 0), rows)
+                lanes = jnp.where(lane3 == x, pltpu.roll(tiles[x], (x - edge) % bz, 1), lanes)
+            faces[kind, side, 0] = rows
+            faces[kind, side, 1] = lanes
 
     def pack_faces(level, source):
         for side, edge in enumerate((bz - 1, 0)):
@@ -267,6 +255,7 @@
 
     halo_w = field_copies(0, w_ref)
     wrow[...] = jnp.zeros_like(wrow)
+    hr[:, :, :, KEEP:ROWS] = jnp.zeros(hr.shape[0:3] + (ROWS - KEEP, bz), f32)
     t0[:, :, 16:24] = jnp.zeros((bx, by, 8, bz), f32)
     split0[96:128] = jnp.zeros((32, split0.shape[1]), bf16)
     split2[96:128] = jnp.zeros((32, split2.shape[1]), bf16)
@@ -302,8 +291,11 @@
     for x in range(bx):
         for d in range(3):
             half = 0.5 * vel[d, x]
-            coef[2 * d, x] = -1.0 - half
-            coef[2 * d + 1, x] = half - 1.0
+            at = (x, row3, lane3)[d]
+            span = (bx, by, bz)[d]
+            coef[2 * d, x] = jnp.where((at == 0) & (place[d] == 0), 0.0, -1.0 - half)
+            coef[2 * d + 1, x] = jnp.where(
+                (at == span - 1) & (place[d] == sizes[d] - 1), 0.0, half - 1.0)
         coef[6, x] = (6.0 - SHIFT) + diag[x]
     zero8 = jnp.zeros((8, 2 * bz), f32)
     for p in range(area // 2):
@@ -328,27 +320,29 @@
         jnp.sum(jnp.where(own8, spread(jnp.where(lane8 < UNIT, unit, 0.0)), 0.0),
                 axis=0, keepdims=True)
         for unit in units], axis=0)
-    gram_state = reduce_start(0, gram_buffers, packed)
-
-    halo_wait(halo_w)
+    gram_state = reduce_start(gram_buffers, packed)
+
+    field_wait(0)
     once = field_stencil(w, 0)
     for x in range(bx):
         image[0, x] = once[x]
     pack_ends(1, once)
+    halo_a = field_copies(1, image.at[0])
+    halo_start(halo_a)
     own = as_row(row_dots(once, first_block))
     squares = sum((tile * tile for tile in once[1:]), once[0] * once[0])
     own = jnp.where(lane1 == KEEP + 1, jnp.sum(
         jnp.sum(squares, axis=0, keepdims=True), axis=1, keepdims=True), own)
-    image_state = reduce_start(3, image_buffers, own)
-    halo_a = field_copies(1, image.at[0])
-    halo_start(halo_a)
+    image_state = reduce_start(image_buffers, own)
     put_row(1, once)
 
-    halo_wait(halo_r)
-    rows_stencil(0, t0, t1)
+    rows_wait(0)
+    halo_t = rows_copies(1, t1)
+    rows_stencil(0, t0, t1, outer)
+    halo_start(halo_t[0:4])
+    rows_stencil(0, t0, t1, inner)
     pack_faces(1, t1)
-    halo_t = rows_copies(1, t1)
-    halo_start(halo_t)
+    halo_start(halo_t[4:6])
     for p in range(area // 2):
         put_split(split1, p, jnp.concatenate(
             both(first_block, p) + both(second_block, p), axis=0))
@@ -360,7 +354,7 @@
     cross = left + pltpu.roll(left, LANES - 48, 1) + jnp.where(
         lane48 < 32, pltpu.roll(left, LANES - 96, 1), pltpu.roll(right, 32, 1))
 
-    halo_wait(halo_a)
+    field_wait(1)
     twice_w = field_stencil(once, 1)
     for x in range(bx):
         image[1, x] = twice_w[x]
@@ -377,13 +371,13 @@
                          pltpu.roll(cross[top:top + 8], (target - source) % LANES, 1), tile)
     for k, col in enumerate(row_dots(twice_w, first_block, second_block)):
         tile = jnp.where(lane8 == 120 + k, col, tile)
-    back_state = reduce_start(1, back_buffers, tile)
+    back_state = reduce_start(back_buffers, tile)
     for p in range(area // 2):
         put_split(split1, p, jnp.concatenate(
             both(first_block, p)[2:3] + both(second_block, p)[0:1], axis=0), 16, 2 * ROWS)
 
-    halo_wait(halo_t)
-    rows_stencil(1, t1, t2)
+    rows_wait(1)
+    rows_stencil(1, t1, t2, outer + inner)
     def third_tail(x, y):
         return third_block(x, y)[0:2] + [t2[x, y, 16:24]
                                          + wrow[(x * by + y) * 8:(x * by + y) * 8 + 8]]
@@ -419,23 +413,23 @@
                 start = start + width
         return tile
 
-    gram_state = reduce_turn(0, gram_buffers, gram_state)
-    image_state = reduce_turn(3, image_buffers, image_state)
+    gram_state = reduce_turn(gram_buffers, gram_state)
+    image_state = reduce_turn(image_buffers, image_state)
     tile = pack_mixed(mixed)
     psend[0] = tile[0:4]
     psend[1] = tile[4:8]
     psend[2] = pack_square(mixed[40:48], square)[0:4]
-    mixed_arrival = exchange(2, psend, precv, 1)
-
-    halo_wait(halo_b)
+    mixed_arrival = exchange(2, 6, psend, precv, 1)
+
+    field_wait(2)
     thrice_w = field_stencil(twice_w, 2)
     put_row(3, thrice_w)
     csend[...] = as_row(row_dots(thrice_w, first_block, second_block, third_block))
-    chain_arrival = exchange(4, csend, crecv, 1)
+    chain_arrival = exchange(3, 7, csend, crecv, 1)
     for x in range(bx):
         for y in range(by):
             out[pl.ds(x * by + y, ROWS, stride=area), :] = t0[x, y]
-    back_state = reduce_turn(1, back_buffers, back_state)
+    back_state = reduce_turn(back_buffers, back_state)
 
     packed = reduce_end(gram_buffers, gram_state)
     units = [
@@ -540,7 +534,7 @@
     own = jnp.where(lane1 < 2 * ROWS, as_row(columns) + q_last * chain_row, 0.0)
     own = jnp.where(lane1 == 2 * ROWS, far_sq, own)
     rsend[...] = own
-    row_state = own, exchange(2, rsend, rrecv, 0)
+    row_state = own, exchange(3, 8, rsend, rrecv, 0)
 
     turn = jnp.where(row < KEEP, -weights, 0.0)
     chain = jnp.where(row8 == 6, (SHIFT - weights[KEEP:KEEP + 1]) * scale,
@@ -618,10 +612,9 @@
     for x in range(bx):
         put_field(KEEP + 2, x, field(q22_col, x))
 
-    for copies in (halo_w, halo_r, halo_a, halo_b, halo_t):
-        halo_finish(copies)
-    for copy in pending[:-1]:
-        copy.wait()
+    for ref, sem in ((hw, halo_send.at[0]), (hr.at[:, :, :, 0:KEEP], halo_send.at[1]), (gslots, red_send.at[0]),
+                     (bslots, red_send.at[1]), (precv, red_send.at[2])):
+        pltpu.make_async_copy(ref, ref, sem).wait()
 
     own = gather_sum(row_state[1], row_state[0], rrecv) * (1.0 / cells)
     y2 = jnp.where(lane1 < 2 * ROWS, y_near + inverse1 * own, 0.0)
@@ -642,7 +635,7 @@
 
     for k in range(EXPAND):
         hess[k:k + 1] = hcols[k]
-    pending[-1].wait()
+    pltpu.make_async_copy(rslots, rslots, red_send.at[3]).wait()
 
 
 def place_results(vectors, columns, out, hess, small, sem):
@@ -666,10 +659,6 @@
     f32 = jnp.float32
     vmem = pl.BlockSpec(memory_space=pltpu.VMEM)
     dma = pltpu.SemaphoreType.DMA
-
-    def buffers(rows):
-        return [pltpu.VMEM((2, rows, LANES), f32), pltpu.VMEM((n0 - 1, rows, LANES), f32),
-                pltpu.VMEM((n1 - 1, rows, LANES), f32)]
 
     vectors, columns = pl.pallas_call(
         functools.partial(body, sizes, cells),
@@ -693,22 +682,19 @@
             pltpu.VMEM((bx, by, ROWS, bz), f32),
             pltpu.VMEM((area * 8, bz), f32),
             pltpu.VMEM((2,) + block, f32),
-            pltpu.VMEM((EXPAND, 2, by, bz), f32),
-            pltpu.VMEM((EXPAND, 2, bx, 1, bz), f32),
-            pltpu.VMEM((EXPAND, 2, by, bz), f32),
-            pltpu.VMEM((EXPAND, 2, by, bz), f32),
-            pltpu.VMEM((2, 2, by, ROWS, bz), f32),
-            pltpu.VMEM((2, 2, bx, ROWS, bz), f32),
-            pltpu.VMEM((2, 2, ROWS, bz), f32),
+            pltpu.VMEM((EXPAND, 2, 3, by, bz), f32),
+            pltpu.VMEM((2, 2, by + bx + 1, ROWS, bz), f32),
+            pltpu.VMEM((EXPAND, 2, 2, by, bz), f32),
             pltpu.VMEM((2, 2, ROWS, bz), f32),
             pltpu.VMEM((128, area * bz), jnp.bfloat16),
             pltpu.VMEM((144, area * bz), jnp.bfloat16),
             pltpu.VMEM((128, area * bz), jnp.bfloat16),
-            *buffers(3), *buffers(8), *buffers(1),
+            pltpu.VMEM((2, 3, LANES), f32), pltpu.VMEM((n0 + n1 - 2, 3, LANES), f32),
+            pltpu.VMEM((2, 8, LANES), f32), pltpu.VMEM((n0 + n1 - 2, 8, LANES), f32),
             pltpu.VMEM((3, 4, LANES), f32), pltpu.VMEM((n1 - 1, 3, 4, LANES), f32),
-            pltpu.VMEM((1, LANES), f32), pltpu.VMEM((n1 - 1, 1, LANES), f32),
-            pltpu.VMEM((1, LANES), f32), pltpu.VMEM((n0 - 1, 1, LANES), f32),
-            dma((5,)), dma((30,)), dma((30,)), dma((10,)), dma((10,)),
+            pltpu.VMEM((2, 1, LANES), f32), pltpu.VMEM((1, LANES), f32),
+            pltpu.VMEM((1, LANES), f32), pltpu.VMEM((2 * (n0 + n1 - 2), 1, LANES), f32),
+            dma((5,)), dma((2,)), dma((5,)), dma((4,)), dma((9,)),
         ],
         compiler_params=pltpu.CompilerParams(collective_id=0, has_side_effects=True),
     )(krylov_basis.reshape(basis, area, bz), schur_vectors.T, next_vector, diag_shift, velocity)

time: 39.2 us -> 38.2 us (0.974)
  Pallas kernels: 38.3 us -> 37.3 us
    pallas_call x1, Pallas kernels: 37.6 us -> 36.6 us  [per_device(): pl.pallas_call(functools.partial(body, sizes, cells), out_shape=(pltpu.VM...]
where the time goes in v4:
time: 38.2 us; the launch traced here: 38 us
  Pallas kernels  37.3 us (98%)
  between operations  0.64 us (2%)
    pallas_call x1, Pallas kernels, per_device(): pl.pallas_call(functools.partial(body, sizes, cells), out_shape=(pltpu.VM...  36.6 us
    pallas_call x1, Pallas kernels, per_device(): pl.pallas_call(place_results, out_shape=(jax.ShapeDtypeStruct((ROWS * are...  0.77 us

profile of v4, /device:TPU:1, one launch (start us, length us, event | category | flops | bytes accessed | tf_op | source)
XLA Modules:
  0.0 38.0 jit_solution(4012878065642837456)
XLA Ops:
  0.6 36.6 %shard_map.68 = (f32[768,128]{1,0:T(8,128)S(1)}, f32[8,128]{1,0:T(8,128)S(1)}) custom-call(f32[60,32,128]{2,1,0:T(8,128)} %bitcast.4, f32[20,60]{1,0:T(8,128)} %bitcast.5, f32[4,8,128]{2,1,0:T(8,128)} %w_hbm.1, f32[4,8,128]{2,1,0:T(8,128)} %diag_hbm.1, f32[3,4,8,128]{3,2,1,0:T(8,128)} %vel_hbm.1), custom_call_target="tpu_custom_call" | custom-call | tf_op jit(solution)/shard_map/pallas_call | solution.py:663
  37.2 0.8 %shard_map.69 = (f32[768,128]{1,0:T(8,128)}, f32[3,24]{1,0:T(4,128)}) custom-call(f32[768,128]{1,0:T(8,128)S(1)} %get-tuple-element.6.vectors, f32[8,128]{1,0:T(8,128)S(1)} %get-tuple-element.7.columns), custom_call_target="tpu_custom_call" | custom-call | tf_op jit(solution)/shard_map/pallas_call | solution.py:702

commit v5 on v4

--- a/solution.py
+++ b/solution.py
@@ -518,8 +518,6 @@
     weigh_chain = q_last * (2.0 * pltpu.roll(jnp.where(lane1 < KEEP, q21, 0.0), 2 * ROWS, 1)
                             + jnp.where(lane1 == KEEP + 2, 2.0 * q_square, 0.0)
                             + jnp.where(lane1 == KEEP + 3, q_last, 0.0))
-    chain_row = gather_sum(chain_arrival, csend[...], crecv)
-    chain_sq = jnp.sum(chain_row * weigh_chain, axis=1, keepdims=True)
     total = gather_sum(mixed_arrival, psend[...], precv)
     tile = jnp.concatenate([total[0], total[1]], axis=0) * weigh_mixed
     last = total[2] * weigh_square
@@ -529,10 +527,13 @@
     columns.append(jnp.concatenate([
         jnp.sum(jnp.where(lane4 < ROWS, last, 0.0), axis=1, keepdims=True),
         jnp.zeros((4, 1), f32)], axis=0))
-    far_sq = chain_sq + jnp.sum(jnp.sum(
-        jnp.where(lane4 < ROWS, 0.0, last), axis=0, keepdims=True), axis=1, keepdims=True)
-    own = jnp.where(lane1 < 2 * ROWS, as_row(columns) + q_last * chain_row, 0.0)
-    own = jnp.where(lane1 == 2 * ROWS, far_sq, own)
+    own = jnp.where(lane1 == 2 * ROWS, jnp.sum(jnp.sum(
+        jnp.where(lane4 < ROWS, 0.0, last), axis=0, keepdims=True), axis=1, keepdims=True),
+        as_row(columns))
+    chain_row = gather_sum(chain_arrival, csend[...], crecv)
+    own = own + jnp.where(
+        lane1 == 2 * ROWS, jnp.sum(chain_row * weigh_chain, axis=1, keepdims=True),
+        jnp.where(lane1 < 2 * ROWS, q_last * chain_row, 0.0))
     rsend[...] = own
     row_state = own, exchange(3, 8, rsend, rrecv, 0)
 
@@ -552,9 +553,11 @@
         far.append(dense)
 
     def combine(columns, x, y):
-        tiles = first_block(x, y) + second_block(x, y)
-        terms = [columns[8 * k:8 * k + 8] * tiles[k] for k in range(6)]
-        v = (terms[0] + terms[1]) + (terms[2] + terms[3]) + (terms[4] + terms[5])
+        tiles = first_block(x, y)
+        if columns.shape[0] > ROWS:
+            tiles = tiles + second_block(x, y)
+        terms = [columns[8 * k:8 * k + 8] * tile for k, tile in enumerate(tiles)]
+        v = sum(terms[1:], terms[0])
         for shift in (4, 2, 1):
             v = v + pltpu.roll(v, shift, 0)
         return v
@@ -611,6 +614,7 @@
     y_near = products(near_col)
     for x in range(bx):
         put_field(KEEP + 2, x, field(q22_col, x))
+    base = [field(near_col, x) + inverse1 * inverse0 * far[x] for x in range(bx)]
 
     for ref, sem in ((hw, halo_send.at[0]), (hr.at[:, :, :, 0:KEEP], halo_send.at[1]), (gslots, red_send.at[0]),
                      (bslots, red_send.at[1]), (precv, red_send.at[2])):
@@ -627,11 +631,12 @@
         assemble(y2, (KEEP + 1, inner[0:1]), (KEEP + 2, inner[1:2]), (ROWS - 1, inner[2:3])),
         gram2, KEEP + 3, True)
     first = jnp.where(row < KEEP, weights, jnp.where(row == KEEP, weights * scale, 0.0))
-    last_col = near_col - jnp.concatenate([first, jnp.zeros((ROWS, LANES), f32)], axis=0)
-    last_col = last_col - weights[KEEP + 1:KEEP + 2] * q21_col
-    last_col = last_col - weights[KEEP + 2:KEEP + 3] * q22_col
     for x in range(bx):
-        put_field(KEEP + 3, x, inverse2 * (field(last_col, x) + inverse1 * inverse0 * far[x]))
+        value = base[x] - field(first, x)
+        for count in (KEEP + 1, KEEP + 2):
+            at = count * area + x * by
+            value = value - weights[count:count + 1] * out[at:at + by, :]
+        put_field(KEEP + 3, x, inverse2 * value)
 
     for k in range(EXPAND):
         hess[k:k + 1] = hcols[k]
@@ -675,7 +680,7 @@
             pltpu.VMEM(block, f32),
             pltpu.VMEM(block, f32),
             pltpu.VMEM((3,) + block, f32),
-            pltpu.VMEM((basis * PITCH, bz), f32),
+            pltpu.VMEM((-(-basis // 8) * 8 * PITCH, bz), f32),
             pltpu.VMEM((7,) + block, f32),
             pltpu.VMEM((bx, by, ROWS, bz), f32),
             pltpu.VMEM((bx, by, ROWS, bz), f32),

time: 38.2 us -> 38 us (level)
  no operation moved by 1% of the time
where the time goes in v5:
time: 38 us; the launch traced here: 37.8 us
  Pallas kernels  37.2 us (98%)
  between operations  0.64 us (2%)
    pallas_call x1, Pallas kernels, per_device(): pl.pallas_call(functools.partial(body, sizes, cells), out_shape=(pltpu.VM...  36.4 us
    pallas_call x1, Pallas kernels, per_device(): pl.pallas_call(place_results, out_shape=(jax.ShapeDtypeStruct((ROWS * are...  0.77 us

profile of v5, /device:TPU:1, one launch (start us, length us, event | category | flops | bytes accessed | tf_op | source)
XLA Modules:
  0.0 37.8 jit_solution(17076225543537666019)
XLA Ops:
  0.6 36.4 %shard_map.68 = (f32[768,128]{1,0:T(8,128)S(1)}, f32[8,128]{1,0:T(8,128)S(1)}) custom-call(f32[60,32,128]{2,1,0:T(8,128)} %bitcast.4, f32[20,60]{1,0:T(8,128)} %bitcast.5, f32[4,8,128]{2,1,0:T(8,128)} %w_hbm.1, f32[4,8,128]{2,1,0:T(8,128)} %diag_hbm.1, f32[3,4,8,128]{3,2,1,0:T(8,128)} %vel_hbm.1), custom_call_target="tpu_custom_call" | custom-call | tf_op jit(solution)/shard_map/pallas_call | solution.py:668
  37.0 0.8 %shard_map.69 = (f32[768,128]{1,0:T(8,128)}, f32[3,24]{1,0:T(4,128)}) custom-call(f32[768,128]{1,0:T(8,128)S(1)} %get-tuple-element.6.vectors, f32[8,128]{1,0:T(8,128)S(1)} %get-tuple-element.7.columns), custom_call_target="tpu_custom_call" | custom-call | tf_op jit(solution)/shard_map/pallas_call | solution.py:707
